TPU v7x, 16 devices: a 4x2x1 block of a 4x4x8 slice. The times are simulated.
16 devices in a mesh: dp: 2 (over y, z), cp: 8 (over x, core).
Axes of the slice: x: 4, y: 2, z: 1, core: 2. Of those that a mesh axis runs over, the one named last changes fastest.
The devices are a block of a 4x4x8 slice.
Arguments:
- hidden: bfloat16 [16384, 2048], P(('dp', 'cp')), parts along dimension 0
- seg_id: int32 [16384], P(('dp', 'cp')), parts along dimension 0
- doc_pos: int32 [16384], P(('dp', 'cp')), parts along dimension 0
- norm_gain: bfloat16 [2048], replicated
- w_qkv: bfloat16 [2048, 2560], replicated
- b_qkv: bfloat16 [2560], replicated
- w_out: bfloat16 [2048, 2048], replicated
- grad_out: bfloat16 [16384, 2048], P(('dp', 'cp')), parts along dimension 0
Outputs:
- output 1: bfloat16 [16384, 2048], P(('dp', 'cp')), parts along dimension 0
- output 2: bfloat16 [16384, 2048], P(('dp', 'cp')), parts along dimension 0
- output 3: float32 [4096], P('dp'), parts along dimension 0
- output 4: float32 [4096, 2560], P('dp'), parts along dimension 0
- output 5: float32 [5120], P('dp'), parts along dimension 0
- output 6: float32 [4096, 2048], P('dp'), parts along dimension 0
There are 2 independent parts. A program takes and returns all parts, laid end to end along the dimension named above; an argument that names none is the same for every part.
All inputs are finite; a program needn't handle non-finite values.
Results may differ from a plain program's by a relative error of at most 0.0188335.
Values are sent between devices in bfloat16 or wider.
A program may use at most 768 MiB of HBM per device.

v0:
```python
import jax
import jax.numpy as jnp
from jax import lax
from jax.sharding import PartitionSpec as P

HEAD_DIM = 128
ROT_DIMS = 64
ROPE_BASE = 5000000.0
EPS_NORM = 1e-5
NEG_BIG = -1e30


def rotate(values, cos_ang, sin_ang):
    rot_pairs = values[..., :ROT_DIMS].reshape(values.shape[:-1] + (ROT_DIMS // 2, 2))
    even_part = rot_pairs[..., 0]
    odd_part = rot_pairs[..., 1]
    turned = jnp.stack([even_part * cos_ang - odd_part * sin_ang, odd_part * cos_ang + even_part * sin_ang], axis=-1)
    return jnp.concatenate([turned.reshape(values.shape[:-1] + (ROT_DIMS,)), values[..., ROT_DIMS:]], axis=-1)


def block_mask(seg_q, seg_k, q_start, k_start):
    q_index = q_start + jnp.arange(seg_q.shape[0])[:, None]
    k_index = k_start + jnp.arange(seg_k.shape[0])[None, :]
    return (seg_q[:, None] == seg_k[None, :]) & (k_index <= q_index)


def forward_update(run_state, q_rot, k_blk, v_blk, vis_mask):
    m_run, l_run, acc_sum = run_state
    scores = jnp.einsum('qgrd,kgd->grqk', q_rot, k_blk, preferred_element_type=jnp.float32) * (HEAD_DIM ** -0.5)
    scores = jnp.where(vis_mask, scores, NEG_BIG)
    m_new = jnp.maximum(m_run, jnp.max(scores, axis=-1))
    p_mat = jnp.where(vis_mask, jnp.exp(scores - m_new[..., None]), 0.0)
    rescale = jnp.exp(m_run - m_new)
    l_new = l_run * rescale + jnp.sum(p_mat, axis=-1)
    acc_new = acc_sum * rescale[..., None] + jnp.einsum('grqk,kgd->grqd', p_mat.astype(jnp.bfloat16), v_blk, preferred_element_type=jnp.float32)
    return m_new, l_new, acc_new


def backward_update(q_rot, k_blk, v_blk, vis_mask, log_norm, grad_ctx, row_dot):
    scale = HEAD_DIM ** -0.5
    scores = jnp.einsum('qgrd,kgd->grqk', q_rot, k_blk, preferred_element_type=jnp.float32) * scale
    p_mat = jnp.where(vis_mask, jnp.exp(jnp.where(vis_mask, scores, NEG_BIG) - log_norm[..., None]), 0.0)
    d_value = jnp.einsum('grqk,grqd->kgd', p_mat.astype(jnp.bfloat16), grad_ctx, preferred_element_type=jnp.float32)
    d_prob = jnp.einsum('grqd,kgd->grqk', grad_ctx, v_blk, preferred_element_type=jnp.float32)
    d_score = (p_mat * (d_prob - row_dot[..., None])).astype(jnp.bfloat16)
    d_query = jnp.einsum('grqk,kgd->qgrd', d_score, k_blk, preferred_element_type=jnp.float32) * scale
    d_key = jnp.einsum('grqk,qgrd->kgd', d_score, q_rot, preferred_element_type=jnp.float32) * scale
    return d_query, d_key, d_value


def solution(mesh):
    n_ctx = mesh.shape['cp']
    shift_perm = [(src_dev, (src_dev + 1) % n_ctx) for src_dev in range(n_ctx)]

    def per_device(hidden, seg_id, doc_pos, norm_gain, w_qkv, b_qkv, w_out, grad_out):
        n_rows, hid_width = hidden.shape
        att_width = w_out.shape[0]
        kv_width = (w_qkv.shape[1] - att_width) // 2
        groups = kv_width // HEAD_DIM
        n_rep = att_width // kv_width
        my_index = lax.axis_index('cp')
        q_start = my_index * n_rows
        hid_f32 = hidden.astype(jnp.float32)
        inv_rms = lax.rsqrt(jnp.mean(hid_f32 * hid_f32, axis=-1, keepdims=True) + EPS_NORM)
        x_hat = hid_f32 * inv_rms
        gain_f32 = norm_gain.astype(jnp.float32)
        normed = (x_hat * gain_f32).astype(jnp.bfloat16)
        qkv_out = (jnp.dot(normed, w_qkv, preferred_element_type=jnp.float32) + b_qkv.astype(jnp.float32)).astype(jnp.bfloat16)
        inv_freq = ROPE_BASE ** (-jnp.arange(0, ROT_DIMS, 2).astype(jnp.float32) / ROT_DIMS)
        angles = doc_pos.astype(jnp.float32)[:, None] * inv_freq[None, :]
        cos_q = jnp.cos(angles)[:, None, None, :]
        sin_q = jnp.sin(angles)[:, None, None, :]
        cos_k = jnp.cos(angles)[:, None, :]
        sin_k = jnp.sin(angles)[:, None, :]
        q_rot = rotate(qkv_out[:, :att_width].astype(jnp.float32).reshape(n_rows, groups, n_rep, HEAD_DIM), cos_q, sin_q).astype(jnp.bfloat16)
        k_rot = rotate(qkv_out[:, att_width:att_width + kv_width].astype(jnp.float32).reshape(n_rows, groups, HEAD_DIM), cos_k, sin_k).astype(jnp.bfloat16)
        v_val = qkv_out[:, att_width + kv_width:].reshape(n_rows, groups, HEAD_DIM)

        def fwd_visit(run_state, k_blk, v_blk, seg_k, src_idx, is_live):
            vis_mask = block_mask(seg_id, seg_k, q_start, src_idx * n_rows)
            return lax.cond(is_live & jnp.any(vis_mask),
                            lambda st_in: forward_update(st_in, q_rot, k_blk, v_blk, vis_mask),
                            lambda st_in: st_in, run_state)

        init_state = (
            jnp.full((groups, n_rep, n_rows), NEG_BIG, jnp.float32),
            jnp.zeros((groups, n_rep, n_rows), jnp.float32),
            jnp.zeros((groups, n_rep, n_rows, HEAD_DIM), jnp.float32),
        )
        run_state = fwd_visit(init_state, k_rot, v_val, seg_id, my_index, True)

        def fwd_turn(turn_idx, loop_vals):
            run_state, k_blk, v_blk, seg_k = loop_vals
            k_blk, v_blk, seg_k = lax.ppermute((k_blk, v_blk, seg_k), 'cp', shift_perm)
            run_state = fwd_visit(run_state, k_blk, v_blk, seg_k, my_index - turn_idx, turn_idx <= my_index)
            return run_state, k_blk, v_blk, seg_k

        run_state = lax.fori_loop(1, n_ctx, fwd_turn, (run_state, k_rot, v_val, seg_id))[0]
        m_run, l_run, acc_sum = run_state
        context = (acc_sum / l_run[..., None]).astype(jnp.bfloat16)
        log_norm = m_run + jnp.log(l_run)
        w_out4 = w_out.reshape(groups, n_rep, HEAD_DIM, hid_width)
        y_out = (hid_f32 + jnp.einsum('grqd,grdn->qn', context, w_out4, preferred_element_type=jnp.float32)).astype(jnp.bfloat16)

        grad_ctx = jnp.einsum('qn,grdn->grqd', grad_out, w_out4, preferred_element_type=jnp.float32).astype(jnp.bfloat16)
        grad_wout = jnp.einsum('grqd,qn->grdn', context, grad_out, preferred_element_type=jnp.float32).reshape(att_width, hid_width)
        row_dot = jnp.einsum('grqd,grqd->grq', grad_ctx, context, preferred_element_type=jnp.float32)

        def bwd_visit(grad_acc, k_blk, v_blk, seg_k, src_idx, is_live):
            vis_mask = block_mask(seg_id, seg_k, q_start, src_idx * n_rows)

            def absorb(acc_in):
                d_query, d_key, d_value = backward_update(q_rot, k_blk, v_blk, vis_mask, log_norm, grad_ctx, row_dot)
                return acc_in[0] + d_query, acc_in[1] + d_key, acc_in[2] + d_value

            return lax.cond(is_live & jnp.any(vis_mask), absorb, lambda acc_in: acc_in, grad_acc)

        zero_kv = jnp.zeros((n_rows, groups, HEAD_DIM), jnp.float32)
        grad_acc = bwd_visit((jnp.zeros((n_rows, groups, n_rep, HEAD_DIM), jnp.float32), zero_kv, zero_kv),
                             k_rot, v_val, seg_id, my_index, True)

        def bwd_turn(turn_idx, loop_vals):
            d_query, d_key, d_value, k_blk, v_blk, seg_k = loop_vals
            k_blk, v_blk, seg_k, d_key, d_value = lax.ppermute((k_blk, v_blk, seg_k, d_key, d_value), 'cp', shift_perm)
            d_query, d_key, d_value = bwd_visit((d_query, d_key, d_value), k_blk, v_blk, seg_k, my_index - turn_idx, turn_idx <= my_index)
            return d_query, d_key, d_value, k_blk, v_blk, seg_k

        d_query, d_key, d_value, _, _, _ = lax.fori_loop(1, n_ctx, bwd_turn, grad_acc + (k_rot, v_val, seg_id))
        d_key, d_value = lax.ppermute((d_key, d_value), 'cp', shift_perm)

        grad_qkv = jnp.concatenate([
            rotate(d_query, cos_q, -sin_q).reshape(n_rows, att_width),
            rotate(d_key, cos_k, -sin_k).reshape(n_rows, kv_width),
            d_value.reshape(n_rows, kv_width)], axis=1).astype(jnp.bfloat16)
        grad_bqkv = jnp.sum(grad_qkv.astype(jnp.float32), axis=0)
        grad_wqkv = jnp.einsum('qn,qc->nc', normed, grad_qkv, preferred_element_type=jnp.float32)
        grad_normed = jnp.einsum('qc,nc->qn', grad_qkv, w_qkv, preferred_element_type=jnp.float32)
        grad_gain = jnp.sum(grad_normed * x_hat, axis=0)
        scaled = grad_normed * gain_f32
        grad_hidden = (grad_out.astype(jnp.float32) + inv_rms * (scaled - x_hat * jnp.mean(scaled * x_hat, axis=-1, keepdims=True))).astype(jnp.bfloat16)
        grad_gain, grad_wqkv, grad_bqkv, grad_wout = lax.psum((grad_gain, grad_wqkv, grad_bqkv, grad_wout), 'cp')
        return y_out, grad_hidden, grad_gain, grad_wqkv, grad_bqkv, grad_wout

    act_spec = P(('dp', 'cp'), None)
    row_spec = P(('dp', 'cp'))
    return jax.shard_map(per_device, mesh=mesh,
                         in_specs=(act_spec, row_spec, row_spec, P(), P(), P(), P(), act_spec),
                         out_specs=(act_spec, act_spec, P('dp'), P('dp', None), P('dp'), P('dp', None)),
                         check_vma=False)
```

profile of v0, /device:TPU:112, one launch (start us, length us, event | category | flops | bytes accessed | tf_op | source)
XLA Modules:
  0.0 2504.0 jit_solution(5609058415097195679)
XLA Ops:
  105.6 92.8 %conditional.4 = (f32[2,8,1024]{2,1,0:T(8,128)}, f32[2,8,1024]{2,1,0:T(8,128)S(1)}, f32[2,8,1024,128]{3,2,1,0:T(8,128)}) conditional(s32[]{:T(128)} %convert_element_type.88, () %tuple.66, (pred[1024,1024]{0,1:T(8,128)(4,1)S(1)}, bf16[1024,2,128]{0,1,2:T(2,128)(2,1)S(1)}, bf16[1024,2,8,128]{0,2,3,1:T(8,128)(2,1)}, ...), branch_computations={%region_2.0_spmd, %region_3.6_spmd} | conditional | flops 8810201088 | bytes 218824736 | solution.py:81
  105.6 38.9 %fusion = (f32[2,8,1024]{2,1,0:T(8,128)S(1)}, f32[2,1024,1024,8]{2,1,3,0:T(8,128)}) fusion(pred[1024,1024]{0,1:T(8,128)(4,1)S(1)} %get-tuple-element.464, bf16[1024,2,8,128]{0,2,3,1:T(8,128)(2,1)} %get-tuple-element.593, bf16[1024,2,128,1]{0,1,2,3:T(2,128)(2,1)S(1)} %bitcast.193), kind=kOutput, calls=%fused_computation.2 | convolution fusion | flops 4345282560 | bytes 72941568 | tf_op jit(solution)/shard_map/cond/branch_1_fun/qgrd,kgd->grqk/dot_general | solution.py:29
  167.0 30.1 %broadcast_add_fusion = f32[2,8,1024,128]{3,2,1,0:T(8,128)} fusion(f32[2,8,1024]{2,1,0:T(8,128)S(1)} %get-tuple-element.683, f32[2,1024,1024,8]{2,1,3,0:T(8,128)} %get-tuple-element.694, f32[2,8,1024]{2,1,0:T(8,128)} %get-tuple-element.905, pred[1024,1024]{0,1:T(8,128)(4,1)S(1)} %get-tuple-element.464, bf16[1024,2,128,1]{2,1,0,3:T(2,128)(2,1)S(1)} %bitcast.207), kind=kOutput, calls=%fused_computation.9 | convolution fusion | flops 4380950528 | bytes 77201408 | tf_op jit(solution)/shard_map/cond/branch_1_fun/grqk,kgd->grqd/dot_general | solution.py:35
  198.4 609.8 %while.46 = (s32[]{:T(128)}, f32[2,8,1024]{2,1,0:T(8,128)}, f32[2,8,1024]{2,1,0:T(8,128)S(1)}, f32[2,8,1024,128]{3,2,1,0:T(8,128)}, bf16[1024,2,128]{2,0,1:T(8,1...) while((s32[]{:T(128)}, f32[2,8,1024]{2,1,0:T(8,128)}, ...), condition=%wide.region_12.13_spmd, body=%wide.region_6.12_spmd.sunk | while | flops 8816461824 | bytes 234930576 | solution.py:98
  215.3 83.7 %collective-permute-start = (s32[1024]{0:T(1024)S(1)}, s32[1024]{0:T(1024)S(1)}, u32[]{:S(2)}, u32[]{:S(2)}) collective-permute-start(s32[1024]{0:T(1024)S(1)} %get-tuple-element.927), channel_id=1, source_target_pairs={{0,1},{1,2},{2,3},{3,4},{4,5},{5,6},{6,7},{7,0},{8,9},{9,10},{10,1... | collective-permute-start | bytes 12296 | tf_op jit(solution)/shard_map/while/body/eval_jaxpr/ppermute | solution.py:94
  316.6 84.6 %collective-permute-start.1 = (bf16[1024,2,128]{2,0,1:T(8,128)(2,1)S(1)}, bf16[1024,2,128]{2,0,1:T(8,128)(2,1)S(1)}, u32[]{:S(2)}, u32[]{:S(2)}) collective-permute-start(bf16[1024,2,128]{2,0,1:T(8,128)(2,1)S(1)} %get-tuple-element.925), channel_id=1, source_target_pairs={{0,1},{1,2},{2,3},{3,4},{4,5},{5,6},{6,7},{7,0},{8,9},{9,10},{10,1... | collective-permute-start | bytes 1572872 | tf_op jit(solution)/shard_map/while/body/eval_jaxpr/ppermute | solution.py:94
  416.4 82.8 %collective-permute-done = s32[1024]{0:T(1024)S(1)} collective-permute-done((s32[1024]{0:T(1024)S(1)}, s32[1024]{0:T(1024)S(1)}, u32[]{:S(2)}, u32[]{:S(2)}) %collective-permute-start) | collective-permute-done | bytes 4128 | tf_op jit(solution)/shard_map/while/body/eval_jaxpr/ppermute | solution.py:94
  517.0 80.3 %collective-permute-done = s32[1024]{0:T(1024)S(1)} collective-permute-done((s32[1024]{0:T(1024)S(1)}, s32[1024]{0:T(1024)S(1)}, u32[]{:S(2)}, u32[]{:S(2)}) %collective-permute-start) | collective-permute-done | bytes 4128 | tf_op jit(solution)/shard_map/while/body/eval_jaxpr/ppermute | solution.py:94
  616.4 79.1 %collective-permute-done = s32[1024]{0:T(1024)S(1)} collective-permute-done((s32[1024]{0:T(1024)S(1)}, s32[1024]{0:T(1024)S(1)}, u32[]{:S(2)}, u32[]{:S(2)}) %collective-permute-start) | collective-permute-done | bytes 4128 | tf_op jit(solution)/shard_map/while/body/eval_jaxpr/ppermute | solution.py:94
  713.9 82.2 %collective-permute-done = s32[1024]{0:T(1024)S(1)} collective-permute-done((s32[1024]{0:T(1024)S(1)}, s32[1024]{0:T(1024)S(1)}, u32[]{:S(2)}, u32[]{:S(2)}) %collective-permute-start) | collective-permute-done | bytes 4128 | tf_op jit(solution)/shard_map/while/body/eval_jaxpr/ppermute | solution.py:94
  819.8 142.2 %conditional.5 = (f32[1024,2,8,128]{3,0,2,1:T(8,128)}, f32[1024,2,128]{2,0,1:T(8,128)}, f32[1024,2,128]{2,0,1:T(8,128)}) conditional(s32[]{:T(128)} %convert_element_type.88, () %tuple.69, (pred[1024,1024]{0,1:T(8,128)(4,1)S(1)}, bf16[1024,2,128]{0,1,2:T(2,128)(2,1)S(1)}, bf16[1024,2,8,128]{0,2,3,1:T(8,128)(2,1)}, f32[2,8,1024]{2,1,0:T(8,128)S(1)}, ...), branch_computations={%region_13.14_spmd, %region_14.15_spmd} | conditional | flops 21678522368 | bytes 342556704 | solution.py:116
  827.1 26.2 %fusion.98 = f32[2,1024,1024,8]{2,1,3,0:T(8,128)} fusion(bf16[1024,2,128,1]{2,0,3,1:T(8,128)(2,1)S(1)} %copy.70, bf16[1024,2,8,128]{3,0,2,1:T(8,128)(2,1)} %copy.50), kind=kOutput, calls=%fused_computation.142 | convolution fusion | flops 4294967296 | bytes 71827456 | tf_op jit(solution)/shard_map/cond/branch_1_fun/qgrd,kgd->grqk/dot_general | solution.py:41
  853.3 26.4 %fusion.37 = f32[1024,2,128]{2,0,1:T(8,128)} fusion(bf16[2,8,1024,128]{2,3,1,0:T(8,128)(2,1)} %get-tuple-element.610, f32[2,1024,1024,8]{2,1,3,0:T(8,128)} %fusion.98, f32[2,8,1024]{2,1,0:T(8,128)S(1)} %get-tuple-element.493, pred[1024,1024]{0,1:T(8,128)(4,1)S(1)} %get-tuple-element.490), kind=kOutput, calls=%fused_computation.46 | convolution fusion | flops 4378853376 | bytes 73465856 | tf_op jit(solution)/shard_map/cond/branch_1_fun/grqk,grqd->kgd/dot_general | solution.py:43
  879.6 43.2 %multiply_convert_fusion = bf16[2,8,1024,1024]{2,3,1,0:T(8,128)(2,1)} fusion(f32[2,1024,1024,8]{2,1,3,0:T(8,128)} %fusion.98, f32[2,8,1024]{2,1,0:T(8,128)} %get-tuple-element.496, f32[2,8,1024]{2,1,0:T(8,128)S(1)} %get-tuple-element.493, pred[1024,1024]{0,1:T(8,128)(4,1)S(1)} %get-tuple-element.490, bf16[2,8,1024,128]{2,3,1,0:T(8,128)(2,1)} %get-tuple-element.610, ...), kind=kOutput, calls=%fused_computation.41 | convolution fusion | flops 4412407808 | bytes 106561536 | tf_op jit(solution)/shard_map/cond/branch_1_fun/grqd,kgd->grqk/dot_general | solution.py:44
  962.0 1082.1 %while.47 = (s32[]{:T(128)}, f32[1024,2,8,128]{3,0,2,1:T(8,128)}, f32[1024,2,128]{2,0,1:T(8,128)}, f32[1024,2,128]{2,0,1:T(8,128)}, bf16[1024,2,128]{2,0,1:T(8,1...) while((s32[]{:T(128)}, f32[1024,2,8,128]{3,0,2,1:T(8,128)}, ...), condition=%wide.region_19.0_spmd, body=%wide.region_15.19_spmd.sunk | while | flops 21685340160 | bytes 363577856 | solution.py:128
  963.4 25.4 %collective-permute-done.3 = s32[1024]{0:T(1024)S(1)} collective-permute-done((s32[1024]{0:T(1024)S(1)}, s32[1024]{0:T(1024)S(1)}, u32[]{:S(2)}, u32[]{:S(2)}) %collective-permute-start.3) | collective-permute-done | bytes 4128 | tf_op jit(solution)/shard_map/while/body/eval_jaxpr/ppermute | solution.py:124
  1002.8 111.6 %collective-permute-start.5 = (f32[1024,2,128]{2,0,1:T(8,128)}, f32[1024,2,128]{2,0,1:T(8,128)S(1)}, u32[]{:S(2)}, u32[]{:S(2)}) collective-permute-start(f32[1024,2,128]{2,0,1:T(8,128)} %get-tuple-element.972), channel_id=1, source_target_pairs={{0,1},{1,2},{2,3},{3,4},{4,5},{5,6},{6,7},{7,0},{8,9},{9,10},{10,1... | collective-permute-start | bytes 3145736 | tf_op jit(solution)/shard_map/while/body/eval_jaxpr/ppermute | solution.py:124
  1176.3 127.5 %collective-permute-start.3 = (s32[1024]{0:T(1024)S(1)}, s32[1024]{0:T(1024)S(1)}, u32[]{:S(2)}, u32[]{:S(2)}) collective-permute-start(s32[1024]{0:T(1024)S(1)} %get-tuple-element.975), channel_id=1, source_target_pairs={{0,1},{1,2},{2,3},{3,4},{4,5},{5,6},{6,7},{7,0},{8,9},{9,10},{10,1... | collective-permute-start | bytes 12296 | tf_op jit(solution)/shard_map/while/body/eval_jaxpr/ppermute | solution.py:124
  1349.8 132.5 %collective-permute-start.7 = (bf16[1024,2,128]{2,0,1:T(8,128)(2,1)}, bf16[1024,2,128]{2,0,1:T(8,128)(2,1)S(1)}, u32[]{:S(2)}, u32[]{:S(2)}) collective-permute-start(bf16[1024,2,128]{2,0,1:T(8,128)(2,1)} %get-tuple-element.974), channel_id=1, source_target_pairs={{0,1},{1,2},{2,3},{3,4},{4,5},{5,6},{6,7},{7,0},{8,9},{9,10},{10,1... | collective-permute-start | bytes 1572872 | tf_op jit(solution)/shard_map/while/body/eval_jaxpr/ppermute | solution.py:124
  1523.4 144.0 %collective-permute-start.6 = (bf16[1024,2,128]{2,0,1:T(8,128)(2,1)}, bf16[1024,2,128]{2,0,1:T(8,128)(2,1)S(1)}, u32[]{:S(2)}, u32[]{:S(2)}) collective-permute-start(bf16[1024,2,128]{2,0,1:T(8,128)(2,1)} %get-tuple-element.973), channel_id=1, source_target_pairs={{0,1},{1,2},{2,3},{3,4},{4,5},{5,6},{6,7},{7,0},{8,9},{9,10},{10,1... | collective-permute-start | bytes 1572872 | tf_op jit(solution)/shard_map/while/body/eval_jaxpr/ppermute | solution.py:124
  1706.9 149.4 %collective-permute-done.3 = s32[1024]{0:T(1024)S(1)} collective-permute-done((s32[1024]{0:T(1024)S(1)}, s32[1024]{0:T(1024)S(1)}, u32[]{:S(2)}, u32[]{:S(2)}) %collective-permute-start.3) | collective-permute-done | bytes 4128 | tf_op jit(solution)/shard_map/while/body/eval_jaxpr/ppermute | solution.py:124
  1882.9 146.9 %collective-permute-done.3 = s32[1024]{0:T(1024)S(1)} collective-permute-done((s32[1024]{0:T(1024)S(1)}, s32[1024]{0:T(1024)S(1)}, u32[]{:S(2)}, u32[]{:S(2)}) %collective-permute-start.3) | collective-permute-done | bytes 4128 | tf_op jit(solution)/shard_map/while/body/eval_jaxpr/ppermute | solution.py:124
  2134.6 27.3 %all-reduce = (f32[2048]{0:T(1024)}, f32[2560]{0:T(1024)}) all-reduce(f32[2048]{0:T(1024)S(1)} %get-tuple-element.627, f32[2560]{0:T(1024)S(1)} %convert_reduce_fusion), channel_id=1, replica_groups=mesh['dp'=2,'cp'=8] {'cp'}, use_global_device_ids=true, to_apply=%region_22.23 | all-reduce | flops 4608 | bytes 36864 | tf_op jit(solution)/shard_map/psum | solution.py:141
  2170.6 301.1 %all-reduce.4.cloned.1.call-done = (f32[2048,2560]{1,0:T(8,128)}, f32[2048,2048]{1,0:T(8,128)}) async-done(((f32[2048,2560]{1,0:T(8,128)}, f32[2048,2048]{1,0:T(8,128)}), (f32[2048,2560]{1,0:T(8,128)}, f32[2048,2048]{1,0:T(8,128)})) %all-reduce.4.cloned.1.call-update) | async-done | bytes 37748752 | tf_op jit(solution)/shard_map/psum | solution.py:141
  (344 shorter events, 654.7 us)
Async XLA Ops:
  7.2 2464.4 %all-reduce.4.cloned.1.call-start = ((), (), s32[]{:S(2)}) async-start(), calls=%async_computation | async-start | bytes 75497472 | tf_op jit(solution)/shard_map/psum | solution.py:141
  1002.8 171.5 %collective-permute-start.5 = (f32[1024,2,128]{2,0,1:T(8,128)}, f32[1024,2,128]{2,0,1:T(8,128)S(1)}, u32[]{:S(2)}, u32[]{:S(2)}) collective-permute-start(f32[1024,2,128]{2,0,1:T(8,128)} %get-tuple-element.972), channel_id=1, source_target_pairs={{0,1},{1,2},{2,3},{3,4},{4,5},{5,6},{6,7},{7,0},{8,9},{9,10},{10,1... | collective-permute-start | bytes 3145736 | tf_op jit(solution)/shard_map/while/body/eval_jaxpr/ppermute | solution.py:124
  1176.3 171.5 %collective-permute-start.5 = (f32[1024,2,128]{2,0,1:T(8,128)}, f32[1024,2,128]{2,0,1:T(8,128)S(1)}, u32[]{:S(2)}, u32[]{:S(2)}) collective-permute-start(f32[1024,2,128]{2,0,1:T(8,128)} %get-tuple-element.972), channel_id=1, source_target_pairs={{0,1},{1,2},{2,3},{3,4},{4,5},{5,6},{6,7},{7,0},{8,9},{9,10},{10,1... | collective-permute-start | bytes 3145736 | tf_op jit(solution)/shard_map/while/body/eval_jaxpr/ppermute | solution.py:124
  1176.3 171.5 %collective-permute-start.4 = (f32[1024,2,128]{2,0,1:T(8,128)}, f32[1024,2,128]{2,0,1:T(8,128)S(1)}, u32[]{:S(2)}, u32[]{:S(2)}) collective-permute-start(f32[1024,2,128]{2,0,1:T(8,128)} %get-tuple-element.971), channel_id=1, source_target_pairs={{0,1},{1,2},{2,3},{3,4},{4,5},{5,6},{6,7},{7,0},{8,9},{9,10},{10,1... | collective-permute-start | bytes 3145736 | tf_op jit(solution)/shard_map/while/body/eval_jaxpr/ppermute | solution.py:124
  1176.3 159.5 %collective-permute-start.3 = (s32[1024]{0:T(1024)S(1)}, s32[1024]{0:T(1024)S(1)}, u32[]{:S(2)}, u32[]{:S(2)}) collective-permute-start(s32[1024]{0:T(1024)S(1)} %get-tuple-element.975), channel_id=1, source_target_pairs={{0,1},{1,2},{2,3},{3,4},{4,5},{5,6},{6,7},{7,0},{8,9},{9,10},{10,1... | collective-permute-start | bytes 12296 | tf_op jit(solution)/shard_map/while/body/eval_jaxpr/ppermute | solution.py:124
  1349.8 171.5 %collective-permute-start.5 = (f32[1024,2,128]{2,0,1:T(8,128)}, f32[1024,2,128]{2,0,1:T(8,128)S(1)}, u32[]{:S(2)}, u32[]{:S(2)}) collective-permute-start(f32[1024,2,128]{2,0,1:T(8,128)} %get-tuple-element.972), channel_id=1, source_target_pairs={{0,1},{1,2},{2,3},{3,4},{4,5},{5,6},{6,7},{7,0},{8,9},{9,10},{10,1... | collective-permute-start | bytes 3145736 | tf_op jit(solution)/shard_map/while/body/eval_jaxpr/ppermute | solution.py:124
  1349.8 171.5 %collective-permute-start.4 = (f32[1024,2,128]{2,0,1:T(8,128)}, f32[1024,2,128]{2,0,1:T(8,128)S(1)}, u32[]{:S(2)}, u32[]{:S(2)}) collective-permute-start(f32[1024,2,128]{2,0,1:T(8,128)} %get-tuple-element.971), channel_id=1, source_target_pairs={{0,1},{1,2},{2,3},{3,4},{4,5},{5,6},{6,7},{7,0},{8,9},{9,10},{10,1... | collective-permute-start | bytes 3145736 | tf_op jit(solution)/shard_map/while/body/eval_jaxpr/ppermute | solution.py:124
  1349.8 159.5 %collective-permute-start.3 = (s32[1024]{0:T(1024)S(1)}, s32[1024]{0:T(1024)S(1)}, u32[]{:S(2)}, u32[]{:S(2)}) collective-permute-start(s32[1024]{0:T(1024)S(1)} %get-tuple-element.975), channel_id=1, source_target_pairs={{0,1},{1,2},{2,3},{3,4},{4,5},{5,6},{6,7},{7,0},{8,9},{9,10},{10,1... | collective-permute-start | bytes 12296 | tf_op jit(solution)/shard_map/while/body/eval_jaxpr/ppermute | solution.py:124
  1349.8 165.1 %collective-permute-start.7 = (bf16[1024,2,128]{2,0,1:T(8,128)(2,1)}, bf16[1024,2,128]{2,0,1:T(8,128)(2,1)S(1)}, u32[]{:S(2)}, u32[]{:S(2)}) collective-permute-start(bf16[1024,2,128]{2,0,1:T(8,128)(2,1)} %get-tuple-element.974), channel_id=1, source_target_pairs={{0,1},{1,2},{2,3},{3,4},{4,5},{5,6},{6,7},{7,0},{8,9},{9,10},{10,1... | collective-permute-start | bytes 1572872 | tf_op jit(solution)/shard_map/while/body/eval_jaxpr/ppermute | solution.py:124
  1523.3 171.5 %collective-permute-start.5 = (f32[1024,2,128]{2,0,1:T(8,128)}, f32[1024,2,128]{2,0,1:T(8,128)S(1)}, u32[]{:S(2)}, u32[]{:S(2)}) collective-permute-start(f32[1024,2,128]{2,0,1:T(8,128)} %get-tuple-element.972), channel_id=1, source_target_pairs={{0,1},{1,2},{2,3},{3,4},{4,5},{5,6},{6,7},{7,0},{8,9},{9,10},{10,1... | collective-permute-start | bytes 3145736 | tf_op jit(solution)/shard_map/while/body/eval_jaxpr/ppermute | solution.py:124
  1523.3 171.5 %collective-permute-start.4 = (f32[1024,2,128]{2,0,1:T(8,128)}, f32[1024,2,128]{2,0,1:T(8,128)S(1)}, u32[]{:S(2)}, u32[]{:S(2)}) collective-permute-start(f32[1024,2,128]{2,0,1:T(8,128)} %get-tuple-element.971), channel_id=1, source_target_pairs={{0,1},{1,2},{2,3},{3,4},{4,5},{5,6},{6,7},{7,0},{8,9},{9,10},{10,1... | collective-permute-start | bytes 3145736 | tf_op jit(solution)/shard_map/while/body/eval_jaxpr/ppermute | solution.py:124
  1523.3 159.5 %collective-permute-start.3 = (s32[1024]{0:T(1024)S(1)}, s32[1024]{0:T(1024)S(1)}, u32[]{:S(2)}, u32[]{:S(2)}) collective-permute-start(s32[1024]{0:T(1024)S(1)} %get-tuple-element.975), channel_id=1, source_target_pairs={{0,1},{1,2},{2,3},{3,4},{4,5},{5,6},{6,7},{7,0},{8,9},{9,10},{10,1... | collective-permute-start | bytes 12296 | tf_op jit(solution)/shard_map/while/body/eval_jaxpr/ppermute | solution.py:124
  1523.3 165.1 %collective-permute-start.7 = (bf16[1024,2,128]{2,0,1:T(8,128)(2,1)}, bf16[1024,2,128]{2,0,1:T(8,128)(2,1)S(1)}, u32[]{:S(2)}, u32[]{:S(2)}) collective-permute-start(bf16[1024,2,128]{2,0,1:T(8,128)(2,1)} %get-tuple-element.974), channel_id=1, source_target_pairs={{0,1},{1,2},{2,3},{3,4},{4,5},{5,6},{6,7},{7,0},{8,9},{9,10},{10,1... | collective-permute-start | bytes 1572872 | tf_op jit(solution)/shard_map/while/body/eval_jaxpr/ppermute | solution.py:124
  1523.4 170.6 %collective-permute-start.6 = (bf16[1024,2,128]{2,0,1:T(8,128)(2,1)}, bf16[1024,2,128]{2,0,1:T(8,128)(2,1)S(1)}, u32[]{:S(2)}, u32[]{:S(2)}) collective-permute-start(bf16[1024,2,128]{2,0,1:T(8,128)(2,1)} %get-tuple-element.973), channel_id=1, source_target_pairs={{0,1},{1,2},{2,3},{3,4},{4,5},{5,6},{6,7},{7,0},{8,9},{9,10},{10,1... | collective-permute-start | bytes 1572872 | tf_op jit(solution)/shard_map/while/body/eval_jaxpr/ppermute | solution.py:124
  1696.8 171.5 %collective-permute-start.5 = (f32[1024,2,128]{2,0,1:T(8,128)}, f32[1024,2,128]{2,0,1:T(8,128)S(1)}, u32[]{:S(2)}, u32[]{:S(2)}) collective-permute-start(f32[1024,2,128]{2,0,1:T(8,128)} %get-tuple-element.972), channel_id=1, source_target_pairs={{0,1},{1,2},{2,3},{3,4},{4,5},{5,6},{6,7},{7,0},{8,9},{9,10},{10,1... | collective-permute-start | bytes 3145736 | tf_op jit(solution)/shard_map/while/body/eval_jaxpr/ppermute | solution.py:124
  1696.8 171.5 %collective-permute-start.4 = (f32[1024,2,128]{2,0,1:T(8,128)}, f32[1024,2,128]{2,0,1:T(8,128)S(1)}, u32[]{:S(2)}, u32[]{:S(2)}) collective-permute-start(f32[1024,2,128]{2,0,1:T(8,128)} %get-tuple-element.971), channel_id=1, source_target_pairs={{0,1},{1,2},{2,3},{3,4},{4,5},{5,6},{6,7},{7,0},{8,9},{9,10},{10,1... | collective-permute-start | bytes 3145736 | tf_op jit(solution)/shard_map/while/body/eval_jaxpr/ppermute | solution.py:124
  1696.8 159.5 %collective-permute-start.3 = (s32[1024]{0:T(1024)S(1)}, s32[1024]{0:T(1024)S(1)}, u32[]{:S(2)}, u32[]{:S(2)}) collective-permute-start(s32[1024]{0:T(1024)S(1)} %get-tuple-element.975), channel_id=1, source_target_pairs={{0,1},{1,2},{2,3},{3,4},{4,5},{5,6},{6,7},{7,0},{8,9},{9,10},{10,1... | collective-permute-start | bytes 12296 | tf_op jit(solution)/shard_map/while/body/eval_jaxpr/ppermute | solution.py:124
  1696.8 165.1 %collective-permute-start.7 = (bf16[1024,2,128]{2,0,1:T(8,128)(2,1)}, bf16[1024,2,128]{2,0,1:T(8,128)(2,1)S(1)}, u32[]{:S(2)}, u32[]{:S(2)}) collective-permute-start(bf16[1024,2,128]{2,0,1:T(8,128)(2,1)} %get-tuple-element.974), channel_id=1, source_target_pairs={{0,1},{1,2},{2,3},{3,4},{4,5},{5,6},{6,7},{7,0},{8,9},{9,10},{10,1... | collective-permute-start | bytes 1572872 | tf_op jit(solution)/shard_map/while/body/eval_jaxpr/ppermute | solution.py:124
  1696.9 170.6 %collective-permute-start.6 = (bf16[1024,2,128]{2,0,1:T(8,128)(2,1)}, bf16[1024,2,128]{2,0,1:T(8,128)(2,1)S(1)}, u32[]{:S(2)}, u32[]{:S(2)}) collective-permute-start(bf16[1024,2,128]{2,0,1:T(8,128)(2,1)} %get-tuple-element.973), channel_id=1, source_target_pairs={{0,1},{1,2},{2,3},{3,4},{4,5},{5,6},{6,7},{7,0},{8,9},{9,10},{10,1... | collective-permute-start | bytes 1572872 | tf_op jit(solution)/shard_map/while/body/eval_jaxpr/ppermute | solution.py:124
  1870.3 171.5 %collective-permute-start.5 = (f32[1024,2,128]{2,0,1:T(8,128)}, f32[1024,2,128]{2,0,1:T(8,128)S(1)}, u32[]{:S(2)}, u32[]{:S(2)}) collective-permute-start(f32[1024,2,128]{2,0,1:T(8,128)} %get-tuple-element.972), channel_id=1, source_target_pairs={{0,1},{1,2},{2,3},{3,4},{4,5},{5,6},{6,7},{7,0},{8,9},{9,10},{10,1... | collective-permute-start | bytes 3145736 | tf_op jit(solution)/shard_map/while/body/eval_jaxpr/ppermute | solution.py:124
  1870.3 171.5 %collective-permute-start.4 = (f32[1024,2,128]{2,0,1:T(8,128)}, f32[1024,2,128]{2,0,1:T(8,128)S(1)}, u32[]{:S(2)}, u32[]{:S(2)}) collective-permute-start(f32[1024,2,128]{2,0,1:T(8,128)} %get-tuple-element.971), channel_id=1, source_target_pairs={{0,1},{1,2},{2,3},{3,4},{4,5},{5,6},{6,7},{7,0},{8,9},{9,10},{10,1... | collective-permute-start | bytes 3145736 | tf_op jit(solution)/shard_map/while/body/eval_jaxpr/ppermute | solution.py:124
  1870.3 159.5 %collective-permute-start.3 = (s32[1024]{0:T(1024)S(1)}, s32[1024]{0:T(1024)S(1)}, u32[]{:S(2)}, u32[]{:S(2)}) collective-permute-start(s32[1024]{0:T(1024)S(1)} %get-tuple-element.975), channel_id=1, source_target_pairs={{0,1},{1,2},{2,3},{3,4},{4,5},{5,6},{6,7},{7,0},{8,9},{9,10},{10,1... | collective-permute-start | bytes 12296 | tf_op jit(solution)/shard_map/while/body/eval_jaxpr/ppermute | solution.py:124
  1870.3 165.1 %collective-permute-start.7 = (bf16[1024,2,128]{2,0,1:T(8,128)(2,1)}, bf16[1024,2,128]{2,0,1:T(8,128)(2,1)S(1)}, u32[]{:S(2)}, u32[]{:S(2)}) collective-permute-start(bf16[1024,2,128]{2,0,1:T(8,128)(2,1)} %get-tuple-element.974), channel_id=1, source_target_pairs={{0,1},{1,2},{2,3},{3,4},{4,5},{5,6},{6,7},{7,0},{8,9},{9,10},{10,1... | collective-permute-start | bytes 1572872 | tf_op jit(solution)/shard_map/while/body/eval_jaxpr/ppermute | solution.py:124
  1870.4 170.6 %collective-permute-start.6 = (bf16[1024,2,128]{2,0,1:T(8,128)(2,1)}, bf16[1024,2,128]{2,0,1:T(8,128)(2,1)S(1)}, u32[]{:S(2)}, u32[]{:S(2)}) collective-permute-start(bf16[1024,2,128]{2,0,1:T(8,128)(2,1)} %get-tuple-element.973), channel_id=1, source_target_pairs={{0,1},{1,2},{2,3},{3,4},{4,5},{5,6},{6,7},{7,0},{8,9},{9,10},{10,1... | collective-permute-start | bytes 1572872 | tf_op jit(solution)/shard_map/while/body/eval_jaxpr/ppermute | solution.py:124
  (63 other events, 2623.4 us)
Sparse Core Ops, SparseCore 0:
  2099.6 372.0 all-reduce.3
where the time goes:
time: 2520 us; the launch traced here: 2500 us
  waiting for transfers between devices  1140 us (45%)
  starting transfers between devices  782 us (31%)
  matrix products  294 us (12%)
  local copies, waits for them, and re-layouts  140 us (6%)
  other arithmetic  95.5 us (4%)
  blocking collectives  27.3 us (1%)
    ppermute x35, starting transfers between devices, bwd_turn(): lax.ppermute((k_blk, v_blk, seg_k, d_key, d_value), 'cp', shift_perm)  585 us
    ppermute x35, waiting for transfers between devices, bwd_turn(): lax.ppermute((k_blk, v_blk, seg_k, d_key, d_value), 'cp', shift_perm)  448 us
    ppermute x21, waiting for transfers between devices, fwd_turn(): k_blk, v_blk, seg_k = lax.ppermute((k_blk, v_blk, seg_k), 'cp', shift_perm)  389 us
    psum x1, waiting for transfers between devices, per_device(): lax.psum((grad_gain, grad_wqkv, grad_bqkv, grad_wout), 'cp')  301 us
    ppermute x21, starting transfers between devices, fwd_turn(): k_blk, v_blk, seg_k = lax.ppermute((k_blk, v_blk, seg_k), 'cp', shift_perm)  197 us
    unnamed x67, local copies, waits for them, and re-layouts  59.1 us
  transfers between devices with their start and end apart: 59, of which 41 were waited for; matrix products, arithmetic and copies ran while one was open for 5% of the time, Pallas kernels for 0%

commit v1 on v0

v1 whole, which is shorter than its diff:
```python
import functools
import math

import jax
import jax.numpy as jnp
import numpy as np
from jax import lax
from jax.experimental import pallas as pl
from jax.experimental.pallas import tpu as pltpu
from jax.sharding import Mesh
from jax.sharding import PartitionSpec as P

HD = 128
ROT_DIMS = 64
ROPE_BASE = 5000000.0
EPS_NORM = 1e-5
NEG = -1e30
CORES = 2
SCALE = HD ** -0.5
CL2 = math.log2(math.e) * SCALE
f32, bf16 = jnp.float32, jnp.bfloat16
BQ, BK, LOOK_F, LOOK_B = 256, 256, 7, 4
VR = HD + 16
RISE = 60.0


def store_off(kb, bk, swap, piece):
    g = kb * bk
    pc = g // piece
    return (pc // 2) * (2 * piece) + ((pc % 2) ^ swap) * piece + g % piece


def visit_blocks(lo, hi, flo, fhi, block):
    @pl.loop(flo, fhi)
    def _(kb):
        block(kb, False)

    @pl.loop(0, (hi - lo) - (fhi - flo))
    def _(j):
        kb = lo + j
        block(jnp.where(kb < flo, kb, kb + (fhi - flo)), True)


def fwd_kernel(meta, q_ref, do_ref, kv_ref, qi_ref, ds_ref, ctx_ref, lse_ref, dd_ref, vt_ref, qt, m_s, mx, acc, vmax, *, nh, piece):
    i = pl.program_id(0)
    swap = meta[4, 0]
    lo, hi, flo, fhi = meta[0, i], meta[1, i], meta[2, i], meta[3, i]
    nk = kv_ref.shape[0]

    @pl.when(i == 0)
    def _():
        tail = jnp.where(lax.broadcasted_iota(jnp.int32, (VR - HD, 512), 0) == 0, 1.0, 0.0).astype(bf16)

        def step(c, m):
            at = pl.ds(pl.multiple_of(c * 512, 512), 512)
            v = kv_ref[at, HD:]
            vt_ref[:HD, at] = v.T
            vt_ref[HD:, at] = tail
            return jnp.maximum(m, jnp.max(jnp.abs(v.astype(f32)).reshape(64, 8, HD), axis=0))
        m = lax.fori_loop(0, nk // 512, step, jnp.zeros((8, HD), f32))
        vmax[...] = jnp.broadcast_to(jnp.max(m, keepdims=True), vmax.shape)

    for h in range(nh):
        qt[h] = q_ref[:, h * HD:(h + 1) * HD].T

    def load(kb):
        off = pl.multiple_of(store_off(kb, BK, swap, piece), BK)
        return kv_ref[pl.ds(off, BK), :HD], vt_ref[:, pl.ds(off, BK)]

    def visible(kb):
        kidx = kb * BK + lax.broadcasted_iota(jnp.int32, (BK, BQ), 0)
        return (kidx >= ds_ref[...]) & (kidx <= qi_ref[...])

    def heads(score, soft, pv):
        sc, pb = {}, {}
        for t in range(nh + LOOK_F + 1):
            if t < nh:
                sc[t] = score(t)
            if t >= LOOK_F + 1:
                pv(t - LOOK_F - 1, pb.pop(t - LOOK_F - 1))
            if LOOK_F <= t < nh + LOOK_F:
                pb[t - LOOK_F] = soft(t - LOOK_F, sc.pop(t - LOOK_F))

    def first(kb):
        kblk, vt = load(kb)
        msk = visible(kb)

        def score(h):
            return jnp.where(msk, jnp.dot(kblk, qt[h], preferred_element_type=f32) * CL2, 2 * NEG)

        def soft(h, s):
            m = jnp.max(s, axis=0, keepdims=True)
            m_s[h:h + 1, :] = m
            mx[h] = jnp.broadcast_to(m, (8, BQ))
            return jnp.exp2(s - m).astype(bf16)

        def pv(h, p):
            acc[h] = jnp.dot(vt, p, preferred_element_type=f32)

        heads(score, soft, pv)

    def block(kb, masked):
        kblk, vt = load(kb)
        msk = visible(kb) if masked else None

        def score(h):
            return jnp.dot(kblk, qt[h], preferred_element_type=f32) * CL2

        def soft(h, s):
            if masked:
                s = jnp.where(msk, s, 2 * NEG)
            mx[h] = jnp.maximum(mx[h], jnp.max(s.reshape(BK // 8, 8, BQ), axis=0))
            return jnp.exp2(s - m_s[h:h + 1, :]).astype(bf16)

        def pv(h, p):
            acc[h] += jnp.dot(vt, p, preferred_element_type=f32)

        heads(score, soft, pv)

    first(hi - 1)
    visit_blocks(lo, hi - 1, jnp.minimum(flo, jnp.minimum(fhi, hi - 1)), jnp.minimum(fhi, hi - 1), block)

    bad = jnp.zeros((8, BQ), f32)
    for h in range(nh):
        bad = jnp.maximum(bad, jnp.where(mx[h] - m_s[h:h + 1, :] <= RISE, 0.0, 1.0))
        bad = jnp.maximum(bad, jnp.where(acc[h, HD:HD + 1, :] * vmax[:1, :] <= 1e37, 0.0, 1.0))

    @pl.when(jnp.max(bad) > 0)
    def _():
        for h in range(nh):
            m_s[h:h + 1, :] = jnp.full((1, BQ), NEG, f32)
            acc[h] = jnp.zeros((VR, BQ), f32)

        @pl.loop(lo, hi)
        def _(kb):
            kblk, vt = load(kb)
            msk = visible(kb)
            for h in range(nh):
                s = jnp.where(msk, jnp.dot(kblk, qt[h], preferred_element_type=f32) * CL2, 2 * NEG)
                m_old = m_s[h:h + 1, :]
                m_new = jnp.maximum(m_old, jnp.max(s, axis=0, keepdims=True))
                m_s[h:h + 1, :] = m_new
                acc[h] = (acc[h] * jnp.exp2(m_old - m_new)
                          + jnp.dot(vt, jnp.exp2(s - m_new).astype(bf16), preferred_element_type=f32))

    for h in range(nh):
        lh = acc[h, HD:HD + 1, :]
        lse_ref[h:h + 1, :] = m_s[h:h + 1, :] + jnp.log2(lh)
        c = acc[h, :HD, :] * (1.0 / lh)
        dot_ = do_ref[:, h * HD:(h + 1) * HD].T.astype(f32)
        dd_ref[h:h + 1, :] = jnp.sum(c * dot_, axis=0, keepdims=True)
        ctx_ref[:, h * HD:(h + 1) * HD] = c.T.astype(bf16)


def resident(shape):
    return pl.BlockSpec(shape, lambda i, m: (0, 0), pipeline_mode=pl.Buffered(1))


def rows_spec(n):
    return pl.BlockSpec((n, BQ), lambda i, m: (0, i))


def flash_fwd(meta, q, do, kv, qi, ds, piece):
    t, w = q.shape
    nh = w // HD
    nk = kv.shape[0]
    tok = pl.BlockSpec((BQ, w), lambda i, m: (i, 0))
    gs = pltpu.PrefetchScalarGridSpec(
        num_scalar_prefetch=1, grid=(t // BQ,),
        in_specs=[tok, tok, resident((nk, 2 * HD)), rows_spec(1), rows_spec(1)],
        out_specs=[tok, rows_spec(nh), rows_spec(nh)],
        scratch_shapes=[pltpu.VMEM((VR, nk), bf16), pltpu.VMEM((nh, HD, BQ), bf16), pltpu.VMEM((nh, BQ), f32), pltpu.VMEM((nh, 8, BQ), f32),
                        pltpu.VMEM((nh, VR, BQ), f32), pltpu.VMEM((8, BQ), f32)])
    return pl.pallas_call(
        functools.partial(fwd_kernel, nh=nh, piece=piece), grid_spec=gs, name='flash_fwd',
        cost_estimate=pl.CostEstimate(flops=4 * t * t * w, bytes_accessed=t * w * 6, transcendentals=0),
        out_shape=[jax.ShapeDtypeStruct((t, w), bf16), jax.ShapeDtypeStruct((nh, t), f32),
                   jax.ShapeDtypeStruct((nh, t), f32)])(meta, q, do, kv, qi, ds)


def bwd_kernel(meta, q_ref, do_ref, kv_ref, qi_ref, ds_ref, lse_ref, dd_ref, tab_ref,
               dq_ref, dkv_ref, kt_ref, qt, dot_, dqa, *, nh, piece):
    i = pl.program_id(0)
    swap = meta[4, 0]

    @pl.when(i == 0)
    def _():
        def step(c, _):
            at = pl.ds(pl.multiple_of(c * 512, 512), 512)
            kt_ref[:, at] = kv_ref[at, :HD].T
            dkv_ref[at, :] = jnp.zeros((512, 2 * HD), f32)
            return 0
        lax.fori_loop(0, kv_ref.shape[0] // 512, step, 0)

    for h in range(nh):
        qt[h] = q_ref[:, h * HD:(h + 1) * HD].T
        dot_[h] = do_ref[:, h * HD:(h + 1) * HD].T
    dqa[...] = jnp.zeros_like(dqa)

    def block(kb, masked):
        off = pl.multiple_of(store_off(kb, BK, swap, piece), BK)
        kblk = kv_ref[pl.ds(off, BK), :HD]
        kt = kt_ref[:, pl.ds(off, BK)]
        vblk = kv_ref[pl.ds(off, BK), HD:]
        if masked:
            kidx = kb * BK + lax.broadcasted_iota(jnp.int32, (BK, BQ), 0)
            msk = (kidx >= ds_ref[...]) & (kidx <= qi_ref[...])
        acc = [None, None]

        def mid(h, s, dp):
            p = jnp.exp2(s * CL2 - lse_ref[h:h + 1, :])
            if masked:
                p = jnp.where(msk, p, 0.0)
            return p.astype(bf16), (p * (dp - dd_ref[h:h + 1, :])).astype(bf16)

        sc, pa = {}, {}
        for t in range(nh + LOOK_B + 1):
            if t < nh:
                sc[t] = (jnp.dot(kblk, qt[t], preferred_element_type=f32),
                         jnp.dot(vblk, dot_[t], preferred_element_type=f32))
            u = t - LOOK_B - 1
            if u >= 0:
                pb, dsb = pa.pop(u)
                t1 = jnp.dot(pb, do_ref[:, u * HD:(u + 1) * HD], preferred_element_type=f32)
                t2 = jnp.dot(dsb, q_ref[:, u * HD:(u + 1) * HD], preferred_element_type=f32)
                acc[0] = t1 if acc[0] is None else acc[0] + t1
                acc[1] = t2 if acc[1] is None else acc[1] + t2
                dqa[u] += jnp.dot(kt, dsb, preferred_element_type=f32)
            if LOOK_B <= t < nh + LOOK_B:
                pa[t - LOOK_B] = mid(t - LOOK_B, *sc.pop(t - LOOK_B))
        dkv_ref[pl.ds(off, BK), :HD] += acc[1]
        dkv_ref[pl.ds(off, BK), HD:] += acc[0]

    visit_blocks(meta[0, i], meta[1, i], meta[2, i], meta[3, i], block)
    ct = tab_ref[:, :HD].T
    even = lax.broadcasted_iota(jnp.int32, (HD, BQ), 0) % 2 == 0
    st = jnp.where(even, tab_ref[:, HD:].T, -tab_ref[:, HD:].T)
    for h in range(nh):
        g = dqa[h] * SCALE
        part = jnp.where(even, pltpu.roll(g, HD - 1, 0), pltpu.roll(g, 1, 0))
        dq_ref[:, h * HD:(h + 1) * HD] = (g * ct + part * st).T.astype(bf16)


def flash_bwd(meta, q, do, kv, qi, ds, lse, dd, tab, piece):
    t, w = q.shape
    nh = w // HD
    nk = kv.shape[0]
    tok = pl.BlockSpec((BQ, w), lambda i, m: (i, 0))
    gs = pltpu.PrefetchScalarGridSpec(
        num_scalar_prefetch=1, grid=(t // BQ,),
        in_specs=[tok, tok, resident((nk, 2 * HD)), rows_spec(1), rows_spec(1),
                  rows_spec(nh), rows_spec(nh), pl.BlockSpec((BQ, 2 * HD), lambda i, m: (i, 0))],
        out_specs=[tok, resident((nk, 2 * HD))],
        scratch_shapes=[pltpu.VMEM((HD, nk), bf16), pltpu.VMEM((nh, HD, BQ), bf16), pltpu.VMEM((nh, HD, BQ), bf16), pltpu.VMEM((nh, HD, BQ), f32)])
    return pl.pallas_call(
        functools.partial(bwd_kernel, nh=nh, piece=piece), grid_spec=gs, name='flash_bwd',
        cost_estimate=pl.CostEstimate(flops=10 * t * t * w, bytes_accessed=t * w * 8, transcendentals=0),
        out_shape=[jax.ShapeDtypeStruct((t, w), bf16), jax.ShapeDtypeStruct((nk, 2 * HD), f32)],
    )(meta, q, do, kv, qi, ds, lse, dd, tab)


MESH = pl.DeviceIdType.MESH


def front_kernel(hid, go, tab, gain_ref, b_ref, rot_ref, w_qkv, w_out,
                 normed, go_o, q_out, gctx_out, kv_all, tab2,
                 hid_v, go_v, tab_v, nrm_v, w_v, wo_v, q_v, gc_v, kv_v,
                 loc, ssem, rsem, ksend, krecv, *, n, nx, aw, kw, att):
    x, k = lax.axis_index('x'), lax.axis_index('k')
    right, left = lax.rem(x + 1, nx), lax.rem(x + nx - 1, nx)
    bar = pltpu.get_barrier_semaphore()
    for peer in ({'k': 1 - k}, {'x': right}, {'x': left}):
        pl.semaphore_signal(bar, inc=1, device_id=peer, device_id_type=MESH)

    kvw = CORES * kw
    col = lambda at, size: w_qkv.at[:, pl.ds(pl.multiple_of(at, HD), size)]
    loads = [pltpu.make_async_copy(hid, hid_v.at[0], loc.at[0]),
             pltpu.make_async_copy(col(att + k * kw, kw), w_v.at[:, aw:aw + kw], loc.at[1]),
             pltpu.make_async_copy(col(att + kvw + k * kw, kw), w_v.at[:, aw + kw:], loc.at[2]),
             pltpu.make_async_copy(tab, tab_v.at[0], loc.at[3]),
             pltpu.make_async_copy(col(k * aw, aw), w_v.at[:, :aw], loc.at[4]),
             pltpu.make_async_copy(go, go_v.at[0], loc.at[5]),
             pltpu.make_async_copy(w_out.at[pl.ds(pl.multiple_of(k * aw, aw), aw), :], wo_v, loc.at[6])]
    for c in loads:
        c.start()
    pl.semaphore_wait(bar, 3)
    give = [pltpu.make_async_remote_copy(src, dst.at[1], ssem.at[i], rsem.at[i], device_id={'k': 1 - k}, device_id_type=MESH)
            for i, (src, dst) in enumerate(((hid, hid_v), (tab, tab_v), (go, go_v)))]
    for c in give:
        c.start()

    gain = gain_ref[...].astype(f32)
    bias = jnp.where(k == 0, b_ref[0:1, :], b_ref[1:2, :])
    rot = rot_ref[...]
    tile = 256
    ntile = n // tile
    full_rows = lambda c, p: pl.ds(pl.multiple_of(c * (2 * n) + p * n, n), n)

    def rope(v, p, r):
        ct = tab_v[p, pl.ds(r, tile), :HD]
        st = tab_v[p, pl.ds(r, tile), HD:]
        return (v.astype(f32) * ct + jnp.dot(v, rot, preferred_element_type=f32) * st).astype(bf16)

    def keys(p):
        def body(t, _):
            r = pl.multiple_of(t * tile, tile)
            h = hid_v[p, pl.ds(r, tile), :].astype(f32)
            inv = lax.rsqrt(jnp.mean(h * h, axis=-1, keepdims=True) + EPS_NORM)
            nv = (h * inv * gain).astype(bf16)
            nrm_v[pl.ds(p * n + r, tile), :] = nv
            kv = (jnp.dot(nv, w_v[:, aw:], preferred_element_type=f32) + bias[:, aw:]).astype(bf16)
            kv_v[pl.ds(p * n + r, tile), :kw] = rope(kv[:, :kw], p, r)
            kv_v[pl.ds(p * n + r, tile), kw:] = kv[:, kw:]
            return 0
        lax.fori_loop(0, ntile, body, 0)

    def queries(p):
        def body(t, _):
            r = pl.multiple_of(t * tile, tile)
            qv = (jnp.dot(nrm_v[pl.ds(p * n + r, tile), :], w_v[:, :aw], preferred_element_type=f32) + bias[:, :aw]).astype(bf16)
            for h in range(aw // HD):
                q_v[pl.ds(p * n + r, tile), h * HD:(h + 1) * HD] = rope(qv[:, h * HD:(h + 1) * HD], p, r)
            return 0
        lax.fori_loop(0, ntile, body, 0)

    def grads(p):
        def body(t, _):
            r = pl.multiple_of(t * tile, tile)
            gc_v[pl.ds(p * n + r, tile), :] = lax.dot_general(
                go_v[p, pl.ds(r, tile), :], wo_v[...], (((1,), (1,)), ((), ())), preferred_element_type=f32).astype(bf16)
            return 0
        lax.fori_loop(0, ntile, body, 0)

    def spread_kv(p):
        out = []
        for d, peer in enumerate((right, left)):
            c = pltpu.make_async_remote_copy(kv_v.at[p * n:(p + 1) * n, :], kv_all.at[full_rows(x, p), :],
                                             ksend.at[2 * p + d], krecv.at[2 * p + d], device_id={'x': peer}, device_id_type=MESH)
            c.start()
            out.append(c)
        return out

    for c in loads[:4]:
        c.wait()
    keys(0)
    sent = spread_kv(0)
    give[0].wait_recv()
    give[1].wait_recv()
    keys(1)
    sent += spread_kv(1)
    stores = [pltpu.make_async_copy(kv_v, kv_all.at[pl.ds(pl.multiple_of(x * (2 * n), 2 * n), 2 * n), :], loc.at[7]),
              pltpu.make_async_copy(nrm_v, normed, loc.at[8]),
              pltpu.make_async_copy(tab_v.at[0], tab2.at[0:n, :], loc.at[9]),
              pltpu.make_async_copy(tab_v.at[1], tab2.at[n:, :], loc.at[10])]
    for c in stores:
        c.start()
    loads[4].wait()
    queries(0)

    sent[0].wait_recv()
    on0 = pltpu.make_async_remote_copy(kv_all.at[full_rows(left, 0), :], kv_all.at[full_rows(left, 0), :],
                                       ksend.at[4], krecv.at[4], device_id={'x': right}, device_id_type=MESH)
    on0.start()
    queries(1)
    stores.append(pltpu.make_async_copy(q_v, q_out, loc.at[11]))
    stores[-1].start()
    sent[3].wait_recv()
    on1 = pltpu.make_async_remote_copy(kv_all.at[full_rows(right, 1), :], kv_all.at[full_rows(right, 1), :],
                                       ksend.at[5], krecv.at[5], device_id={'x': left}, device_id_type=MESH)
    on1.start()
    loads[5].wait()
    loads[6].wait()
    grads(0)
    give[2].wait_recv()
    stores.append(pltpu.make_async_copy(go_v.at[1], go_o, loc.at[12]))
    stores[-1].start()
    grads(1)
    stores.append(pltpu.make_async_copy(gc_v, gctx_out, loc.at[13]))
    stores[-1].start()
    for c in stores:
        c.wait()
    for c in give:
        c.wait_send()
    sent[1].wait_recv()
    sent[2].wait_recv()
    for c in sent:
        c.wait_send()
    on0.wait()
    on1.wait()


def front(hidden, grad_out, tab, norm_gain, bias, rot, w_qkv, w_out, nx, kw):
    n, d = hidden.shape
    att = w_out.shape[0]
    aw = att // CORES
    hbm = pl.BlockSpec(memory_space=pl.ANY)
    vmem = pl.BlockSpec(memory_space=pltpu.VMEM)
    sds = jax.ShapeDtypeStruct
    dma = pltpu.SemaphoreType.DMA
    return pl.pallas_call(
        functools.partial(front_kernel, n=n, nx=nx, aw=aw, kw=kw, att=att), name='front',
        in_specs=[hbm, hbm, hbm, vmem, vmem, vmem, hbm, hbm], out_specs=[hbm] * 6,
        out_shape=[sds((2 * n, d), bf16), sds((n, d), bf16), sds((2 * n, aw), bf16), sds((2 * n, aw), bf16),
                   sds((nx * 2 * n, 2 * kw), bf16), sds((2 * n, 2 * HD), f32)],
        scratch_shapes=[pltpu.VMEM((2, n, d), bf16), pltpu.VMEM((2, n, d), bf16), pltpu.VMEM((2, n, 2 * HD), f32),
                        pltpu.VMEM((2 * n, d), bf16), pltpu.VMEM((d, aw + 2 * kw), bf16), pltpu.VMEM((aw, d), bf16),
                        pltpu.VMEM((2 * n, aw), bf16), pltpu.VMEM((2 * n, aw), bf16), pltpu.VMEM((2 * n, 2 * kw), bf16),
                        dma((14,)), dma((3,)), dma((3,)), dma((6,)), dma((6,))],
        compiler_params=pltpu.CompilerParams(collective_id=0, has_side_effects=True, vmem_limit_bytes=60 << 20),
        cost_estimate=pl.CostEstimate(flops=60 * 10 ** 9, bytes_accessed=50 * 10 ** 6, transcendentals=0),
    )(hidden, grad_out, tab, norm_gain, bias, rot, w_qkv, w_out)


def block_table(qi, ds, swap):
    q2, d2 = qi.reshape(-1, BQ), ds.reshape(-1, BQ)
    lo = d2[:, 0] // BK
    hi = q2[:, -1] // BK + 1
    flo = jnp.minimum((d2[:, -1] + BK - 1) // BK, hi)
    fhi = jnp.maximum((q2[:, 0] + 1) // BK, flo)
    return jnp.stack([lo, hi, flo, fhi, jnp.full_like(lo, swap)]).astype(jnp.int32)


def pair_swap():
    r = np.zeros((HD, HD), np.float32)
    for j in range(ROT_DIMS // 2):
        r[2 * j + 1, 2 * j] = -1.0
        r[2 * j, 2 * j + 1] = 1.0
    return r


def solution(mesh):
    axes = dict(mesh.shape)
    mesh3 = Mesh(mesh.devices.reshape(axes['dp'], axes['cp'] // CORES, CORES), ('dp', 'x', 'k'))
    flip = [(0, 1), (1, 0)]
    nx = mesh3.shape['x']

    def per_device(hidden, seg_id, doc_pos, norm_gain, w_qkv, b_qkv, w_out, grad_out):
        n, d = hidden.shape
        att = w_out.shape[0]
        kvw = (w_qkv.shape[1] - att) // 2
        aw, kw = att // CORES, kvw // CORES
        x, k = lax.axis_index('x'), lax.axis_index('k')
        other = lambda a: lax.ppermute(a, 'k', flip)
        both = lambda a: jnp.concatenate([a, other(a)], axis=0)

        pos2 = both(doc_pos)
        base = x * (CORES * n)
        qi = jnp.concatenate([base + k * n + jnp.arange(n), base + (1 - k) * n + jnp.arange(n)]).astype(jnp.int32)
        ds = qi - pos2
        meta = block_table(qi, ds, k)

        def cols(w, c):
            part = lambda a, b: lax.dynamic_slice_in_dim(w, a, b, axis=-1)
            return jnp.concatenate([part(c * aw, aw), part(att + c * kw, kw), part(att + kvw + c * kw, kw)], axis=-1)

        inv_freq = ROPE_BASE ** (-jnp.arange(0, ROT_DIMS, 2).astype(f32) / ROT_DIMS)
        ang = inv_freq[:, None] * doc_pos.astype(f32)[None, :]
        wide = lambda a, fill: jnp.concatenate([jnp.repeat(a, 2, axis=0), jnp.full((HD - ROT_DIMS, n), fill, f32)], axis=0)
        tab = jnp.concatenate([wide(jnp.cos(ang), 1.0), wide(jnp.sin(ang), 0.0)], axis=0).T
        bias = jnp.stack([jnp.concatenate([b_qkv[c * aw:(c + 1) * aw], b_qkv[att + c * kw:att + (c + 1) * kw],
                                           b_qkv[att + kvw + c * kw:att + kvw + (c + 1) * kw]]) for c in range(CORES)]).astype(f32)
        gain = norm_gain.astype(f32)
        normed, go_o, q, gctx, kv_all, tab2 = front(hidden, grad_out, tab, norm_gain[None], bias,
                                                     jnp.asarray(pair_swap(), bf16), w_qkv, w_out, nx, kw)
        w_me, w_ot = cols(w_qkv, k), cols(w_qkv, 1 - k)
        wo_me = lax.dynamic_slice_in_dim(w_out, k * aw, aw, axis=0)
        wo_ot = lax.dynamic_slice_in_dim(w_out, (1 - k) * aw, aw, axis=0)
        ctx, lse, dd = flash_fwd(meta, q, gctx, kv_all, qi[None], ds[None], n)
        over = (((0,), (0,)), ((), ()))
        g_wout = (lax.dot_general(ctx[:n], grad_out, over, preferred_element_type=f32)
                  + lax.dot_general(ctx[n:], go_o, over, preferred_element_type=f32))
        lse, g_wout = lax.optimization_barrier((lse, g_wout))
        g_wout = lax.psum(g_wout, 'x')
        ctx_o = other(ctx[n:])
        y_out = (hidden.astype(f32) + jnp.dot(ctx[:n], wo_me, preferred_element_type=f32)
                 + jnp.dot(ctx_o, wo_ot, preferred_element_type=f32)).astype(bf16)

        dq, dkv = flash_bwd(meta, q, gctx, kv_all, qi[None], ds[None], lse, dd, tab2, n)
        c_tok, s_tok = tab2[:, :HD], tab2[:, HD:]
        dkv, g_wout = lax.optimization_barrier((dkv, g_wout))
        wout_o = other(g_wout)
        o_wout = jnp.where(k == 0, jnp.concatenate([g_wout, wout_o]), jnp.concatenate([wout_o, g_wout]))
        dkv = lax.psum_scatter(dkv, 'x', scatter_dimension=0, tiled=True)
        dk = dkv[:, :kw] * SCALE
        dkt = jnp.dot(dk, jnp.asarray(pair_swap().T), precision=lax.Precision.HIGHEST, preferred_element_type=f32)
        gqkv = jnp.concatenate([dq, (dk * c_tok + dkt * s_tok).astype(bf16), dkv[:, kw:].astype(bf16)], axis=1)
        g_wqkv = lax.dot_general(normed, gqkv, (((0,), (0,)), ((), ())), preferred_element_type=f32)
        g_wqkv = lax.psum_scatter(g_wqkv, 'x', scatter_dimension=0, tiled=True)
        g_wqkv = lax.all_gather(g_wqkv, ('x', 'k'), axis=0)
        g_wqkv = g_wqkv.reshape(-1, CORES, *g_wqkv.shape[1:])
        two = lambda a, b: [g_wqkv[:, c, :, a:b] for c in range(CORES)]
        o_wqkv = jnp.concatenate(two(0, aw) + two(aw, aw + kw) + two(aw + kw, aw + 2 * kw), axis=-1).reshape(w_qkv.shape)
        gq_o = other(gqkv[n:])
        dims = (((1,), (1,)), ((), ()))
        gnorm = (lax.dot_general(gqkv[:n], w_me, dims, preferred_element_type=f32)
                 + lax.dot_general(gq_o, w_ot, dims, preferred_element_type=f32))
        h32 = hidden.astype(f32)
        inv_rms = lax.rsqrt(jnp.mean(h32 * h32, axis=-1, keepdims=True) + EPS_NORM)
        x_hat = h32 * inv_rms
        g_gain = jnp.sum(gnorm * x_hat, axis=0)
        scaled = gnorm * gain
        g_hidden = (grad_out.astype(f32) + inv_rms * (scaled - x_hat * jnp.mean(scaled * x_hat, axis=-1, keepdims=True))).astype(bf16)
        g_b = jnp.sum(gqkv.astype(f32), axis=0)
        g_gain = lax.psum(g_gain, ('x', 'k'))
        g_b = lax.psum(g_b, 'x')

        def join(out, mine, c):
            put = lambda o, v, at: lax.dynamic_update_slice_in_dim(o, v, at, axis=-1)
            out = put(out, mine[..., :aw], c * aw)
            out = put(out, mine[..., aw:aw + kw], att + c * kw)
            return put(out, mine[..., aw + kw:], att + kvw + c * kw)

        full = lambda shape: jnp.zeros(shape, f32)
        o_b = join(join(full(b_qkv.shape), g_b, k), other(g_b), 1 - k)
        return y_out, g_hidden, g_gain, o_wqkv, o_b, o_wout

    act = P(('dp', 'x', 'k'), None)
    row = P(('dp', 'x', 'k'))
    return jax.shard_map(per_device, mesh=mesh3,
                         in_specs=(act, row, row, P(), P(), P(), P(), act),
                         out_specs=(act, act, P('dp'), P('dp', None), P('dp'), P('dp', None)),
                         check_vma=False)
```

time: 2520 us -> 680 us (0.27)
  waiting for transfers between devices: 1140 us -> 339 us
  starting transfers between devices: 782 us -> 1.53 us
  matrix products: 294 us -> 77.4 us
  Pallas kernels: 0 us -> 151 us
  local copies, waits for them, and re-layouts: 140 us -> 43.3 us
  other arithmetic: 95.5 us -> 33.4 us
    ppermute x58 -> x5, waiting for transfers between devices: 837 us -> 0.01 us  [per_device(): other = lambda a: lax.ppermute(a, 'k', flip)]
    ppermute x58 -> x5, starting transfers between devices: 782 us -> 1.27 us  [per_device(): other = lambda a: lax.ppermute(a, 'k', flip)]
    dot_general x13 -> x8, matrix products: 294 us -> 77.4 us  [the longest x1 16.1 us: per_device(): lax.dot_general(normed, gqkv, (((0,), (0,)), ((), ())), preferred_element...]
    reduce_scatter x0 -> x2, waiting for transfers between devices: none -> 197 us  [the longest x1 103 us: per_device(): dkv = lax.psum_scatter(dkv, 'x', scatter_dimension=0, tiled=True)]
    psum x1, waiting for transfers between devices: 301 us -> 142 us  [per_device(): g_wout = lax.psum(g_wout, 'x')]
    pallas_call x0 -> x3, Pallas kernels: none -> 151 us  [the longest x1 66.3 us: flash_bwd(): pl.pallas_call(functools.partial(bwd_kernel, nh=nh, piece=piece), grid_sp...]
    while x62 -> x0, local copies, waits for them, and re-layouts: 56 us -> none
    unnamed x67 -> x39, local copies, waits for them, and re-layouts: 59.1 us -> 14 us
  transfers between devices with their start and end apart: 59 -> 9, of which waited for: 41 -> 3; matrix products, arithmetic and copies ran while one was open for 5% -> 13% of each run, Pallas kernels for 0% -> 17%
where the time goes in v1:
time: 680 us; the launch traced here: 685 us
  waiting for transfers between devices  339 us (50%)
  Pallas kernels  151 us (22%)
  matrix products  77.4 us (11%)
  local copies, waits for them, and re-layouts  43.3 us (6%)
  other arithmetic  33.4 us (5%)
  blocking collectives  24.6 us (4%)
  between operations  14.7 us (2%)
    psum x1, waiting for transfers between devices, per_device(): g_wout = lax.psum(g_wout, 'x')  142 us
    reduce_scatter x1, waiting for transfers between devices, per_device(): dkv = lax.psum_scatter(dkv, 'x', scatter_dimension=0, tiled=True)  103 us
    reduce_scatter x1, waiting for transfers between devices, per_device(): g_wqkv = lax.psum_scatter(g_wqkv, 'x', scatter_dimension=0, tiled=True)  93.2 us
    pallas_call x1, Pallas kernels, flash_bwd(): pl.pallas_call(functools.partial(bwd_kernel, nh=nh, piece=piece), grid_sp...  66.3 us
    pallas_call x1, Pallas kernels, front(): pl.pallas_call(functools.partial(front_kernel, n=n, nx=nx, aw=aw, kw=kw,...  47.2 us
    pallas_call x1, Pallas kernels, flash_fwd(): pl.pallas_call(functools.partial(fwd_kernel, nh=nh, piece=piece), grid_sp...  37.5 us
    dot_general x1, matrix products, per_device(): lax.dot_general(normed, gqkv, (((0,), (0,)), ((), ())), preferred_element...  16.1 us
    psum x1, blocking collectives, per_device(): g_gain = lax.psum(g_gain, ('x', 'k'))  15.6 us
  transfers between devices with their start and end apart: 9, of which 3 were waited for; matrix products, arithmetic and copies ran while one was open for 13% of the time, Pallas kernels for 17%

profile of v1, /device:TPU:112, one launch (start us, length us, event | category | flops | bytes accessed | tf_op | source)
XLA Modules:
  0.0 685.1 jit_solution(1214503535316713577)
XLA Ops:
  14.9 47.2 %front.1 = (bf16[2048,2048]{1,0:T(8,128)(2,1)}, bf16[1024,2048]{1,0:T(8,128)(2,1)}, bf16[2048,1024]{1,0:T(8,128)(2,1)}, bf16[2048,1024]{1,0:T(8,128)(2,1)}, bf16...) custom-call(bf16[1024,2048]{1,0:T(8,128)(2,1)} %hid.1, bf16[1024,2048]{1,0:T(8,128)(2,1)} %go.1, ...), custom_call_target="tpu_custom_call" | custom-call | flops 60000002048 | bytes 50000000 | tf_op jit(solution)/shard_map/front/pallas_call | solution.py:400
  63.8 37.5 %flash_fwd.1 = (bf16[2048,1024]{1,0:T(8,128)(2,1)}, f32[8,2048]{1,0:T(8,128)}, f32[8,2048]{1,0:T(8,128)}) custom-call(s32[5,8]{1,0:T(8,128)} %stack.16.meta, bf16[2048,1024]{1,0:T(8,128)(2,1)} %get-tuple-element.21.q_ref, bf16[2048,1024]{1,0:T(8,128)(2,1)} %get-tuple-element.22.do_ref, bf16[8192,256]{1,0:T(8,128)(2,1)} %get-tuple-element.23.kv_ref, ...), custom_call_target="tpu_custom_call" | custom-call | flops 17179869184 | bytes 12582912 | tf_op jit(solution)/shard_map/flash_fwd/pallas_call | solution.py:174
  101.3 7.8 %fusion.36 = f32[1024,2048]{1,0:T(8,128)S(1)} fusion(bf16[1024,2048]{1,0:T(8,128)(2,1)} %go.1, bf16[2048,1024]{1,0:T(8,128)(2,1)} %get-tuple-element.24), kind=kOutput, calls=%fused_computation.40 | convolution fusion | flops 4294967296 | bytes 14680064 | tf_op jit(solution)/shard_map/dot_general | solution.py:470
  109.2 7.3 %convolution_add_fusion = f32[1024,2048]{1,0:T(8,128)} fusion(f32[1024,2048]{1,0:T(8,128)S(1)} %fusion.36, bf16[1024,2048]{1,0:T(8,128)(2,1)S(1)} %copy-done.12, bf16[2048,1024]{1,0:T(8,128)(2,1)S(1)} %copy-done.4), kind=kOutput, calls=%fused_computation.35 | convolution fusion | flops 4297064448 | bytes 23068672 | tf_op jit(solution)/shard_map/dot_general | solution.py:471
  116.6 66.3 %flash_bwd.1 = (bf16[2048,1024]{1,0:T(8,128)(2,1)}, f32[8192,256]{1,0:T(8,128)}) custom-call(s32[5,8]{1,0:T(8,128)} %stack.16.meta, bf16[2048,1024]{1,0:T(8,128)(2,1)} %get-tuple-element.21.q_ref, bf16[2048,1024]{1,0:T(8,128)(2,1)} %get-tuple-element.22.do_ref, bf16[8192,256]{1,0:T(8,128)(2,1)} %get-tuple-element.23.kv_ref, s32[1,2048]{1,0:T(1,128)} %bitcast.80, ...), custom_call_target="tpu_custom_call" | custom-call | flops 42949672960 | bytes 16777216 | tf_op jit(solution)/shard_map/flash_bwd/pallas_call | solution.py:255
  182.9 142.2 %all-reduce.2.cloned.1.call-done = f32[1024,2048]{1,0:T(8,128)} async-done(((f32[1024,2048]{1,0:T(8,128)}), f32[1024,2048]{1,0:T(8,128)}) %all-reduce.2.cloned.1.call-update) | async-done | bytes 8388624 | tf_op jit(solution)/shard_map/psum | solution.py:473
  325.3 103.5 %reduce-scatter.3.cloned.1.call-done = f32[2048,256]{1,0:T(8,128)} async-done(((f32[8192,256]{1,0:T(8,128)}), f32[2048,256]{1,0:T(8,128)}) %reduce-scatter.3.cloned.1.call-update) | async-done | bytes 2097168 | tf_op jit(solution)/shard_map/reduce_scatter | solution.py:483
  432.7 3.9 convert_reduce_fusion
  438.9 16.1 %fusion.63 = f32[2048,1280]{1,0:T(8,128)} fusion(bf16[2048,2048]{1,0:T(8,128)(2,1)} %get-tuple-element.34, bf16[2048,1280]{1,0:T(8,128)(2,1)S(1)} %get-tuple-element.43), kind=kOutput, calls=%fused_computation.127 | convolution fusion | flops 10737418240 | bytes 24117248 | tf_op jit(solution)/shard_map/dot_general | solution.py:487
  455.1 93.2 %reduce-scatter.5.cloned.1.call-done = f32[512,1280]{1,0:T(8,128)} async-done(((f32[2048,1280]{1,0:T(8,128)}), f32[512,1280]{1,0:T(8,128)}) %reduce-scatter.5.cloned.1.call-update) | async-done | bytes 2621456 | tf_op jit(solution)/shard_map/reduce_scatter | solution.py:488
  550.9 3.1 fusion.11
  553.9 2.8 constant_dynamic-slice_fusion.1
  556.7 8.0 %constant_dynamic-slice_fusion.2 = (bf16[2048,1024]{1,0:T(8,128)(2,1)}, bf16[2048,1024]{1,0:T(8,128)(2,1)}) fusion(bf16[2048,2560]{1,0:T(8,128)(2,1)} %w_qkv.1, s32[]{:T(128)S(6)} %select_n.101, s32[]{:T(128)S(6)} %select_n.98), kind=kLoop, calls=%fused_computation.85 | loop fusion | bytes 16777224 | tf_op jit(solution)/shard_map/dynamic_slice | solution.py:453
  564.7 9.3 %fusion.29 = f32[1024,2048]{1,0:T(8,128)} fusion(bf16[2048,2048]{1,0:T(8,128)(2,1)} %w_out.1, s32[]{:T(128)S(6)} %select_n.96, bf16[2048,1024]{1,0:T(8,128)(2,1)S(1)} %copy-done.5), kind=kOutput, calls=%fused_computation.33 | convolution fusion | flops 4294967296 | bytes 14680068 | tf_op jit(solution)/shard_map/dot_general | solution.py:475
  574.0 12.1 %fusion.10 = bf16[1024,2048]{1,0:T(8,128)(2,1)} fusion(f32[1024,2048]{1,0:T(8,128)} %fusion.29, bf16[1024,2048]{1,0:T(8,128)(2,1)S(1)} %copy-done, bf16[1024,1024]{1,0:T(8,128)(2,1)} %collective-permute-done.1, bf16[2048,2048]{1,0:T(8,128)(2,1)} %w_out.1, s32[]{:T(128)S(6)} %select_n.97), kind=kOutput, calls=%fused_computation.15 | convolution fusion | flops 4303355904 | bytes 23068676 | tf_op jit(solution)/shard_map/dot_general | solution.py:476
  586.1 13.2 %maximum_select_fusion = f32[2048,2048]{1,0:T(8,128)} fusion(f32[1024,2048]{1,0:T(8,128)} %collective-permute-done.4, f32[1024,2048]{1,0:T(8,128)S(1)} %bitcast.70, pred[]{:T(512)S(6)} %eq.3), kind=kLoop, calls=%fused_computation | loop fusion | flops 12582912 | bytes 33554432 | tf_op jit(solution)/shard_map/jit(_where)/select_n | solution.py:482
  599.5 9.1 %psum.23 = f32[1280]{0:T(1024)S(1)} all-reduce(f32[1280]{0:T(1024)S(1)} %get-tuple-element.42), channel_id=1, replica_groups=mesh['dp'=2,'x'=4,'k'=2] {'x'}, use_global_device_ids=true, to_apply=%region_8.9 | all-reduce | flops 1280 | bytes 10240 | tf_op jit(solution)/shard_map/psum | solution.py:505
  609.3 10.6 %fusion.12 = f32[1024,2048]{1,0:T(8,128)} fusion(bf16[2048,128]{1,0:T(8,128)(2,1)} %get-tuple-element.55, bf16[2048,128]{1,0:T(8,128)(2,1)} %get-tuple-element.56, bf16[2048,1024]{1,0:T(8,128)(2,1)} %get-tuple-element.53, bf16[2048,1280]{1,0:T(8,128)(2,1)} %copy-done.2), kind=kOutput, calls=%fused_computation.18 | convolution fusion | flops 5384437760 | bytes 16252928 | tf_op jit(solution)/shard_map/dot_general | solution.py:495
  620.3 11.5 %fusion.8 = (f32[2048]{0:T(1024)S(1)}, f32[1024]{0:T(1024)S(1)}, f32[1024,2048]{1,0:T(8,128)}) fusion(bf16[1024,2048]{1,0:T(8,128)(2,1)S(1)} %copy-done.1, f32[1024]{0:T(1024)S(1)} %add_rsqrt_fusion, f32[2048]{0:T(1024)S(1)} %convert_element_type.43, f32[1024,2048]{1,0:T(8,128)} %fusion.12, bf16[1024,1280]{1,0:T(8,128)(2,1)S(1)} %collective-permute-done.2, ...), kind=kOutput, calls=%fused_computation.13 | convolution fusion | flops 5401211904 | bytes 28860416 | tf_op jit(solution)/shard_map/dot_general | solution.py:496
  631.8 15.6 %psum.22 = f32[2048]{0:T(1024)} all-reduce(f32[2048]{0:T(1024)S(1)} %get-tuple-element.36), channel_id=1, replica_groups=mesh['dp'=2,'x'=4,'k'=2] {'x','k'}, use_global_device_ids=true, to_apply=%region_5.6 | all-reduce | flops 2048 | bytes 16384 | tf_op jit(solution)/shard_map/psum | solution.py:504
  647.4 8.7 %fusion.7 = bf16[1024,2048]{1,0:T(8,128)(2,1)} fusion(bf16[1024,2048]{1,0:T(8,128)(2,1)} %hid.1, bf16[1024,2048]{1,0:T(8,128)(2,1)} %go.1, f32[1024,2048]{1,0:T(8,128)} %get-tuple-element.67, f32[1024]{0:T(1024)S(1)} %broadcast_multiply_fusion, f32[2048]{0:T(1024)S(1)} %convert_element_type.43, f32[1024]{0:T(1024)S(1)} %add_rsqrt_fusion), kind=kLoop, calls=%fused_computation.12 | loop fusion | flops 18874368 | bytes 20987904 | tf_op jit(solution)/shard_map/convert_element_type | solution.py:502
  658.6 6.8 fusion.60
  665.4 4.2 constant_dynamic-update-slice_fusion.5
  669.7 4.2 constant_dynamic-update-slice_fusion.4
  (108 shorter events, 26.3 us)
Async XLA Ops:
  7.2 318.0 %all-reduce.2.cloned.1.call-start = ((), (), s32[]{:S(2)}) async-start(), calls=%async_computation.2 | async-start | bytes 16777216 | tf_op jit(solution)/shard_map/psum | solution.py:473
  7.2 55.1 %collective-permute-start = (s32[1024]{0:T(1024)}, s32[1024]{0:T(1024)S(1)}, u32[]{:S(2)}, u32[]{:S(2)}) collective-permute-start(s32[1024]{0:T(1024)} %param.11), channel_id=1, source_target_pairs={{0,1},{1,0},{2,3},{3,2},{4,5},{5,4},{6,7},{7,6},{8,9},{9,8},{10,11... | collective-permute-start | bytes 12296 | tf_op jit(solution)/shard_map/ppermute | solution.py:443
  14.9 47.2 %copy-start.9 = (s32[1024]{0:T(1024)S(1)}, s32[1024]{0:T(1024)}, u32[]{:S(2)}) copy-start(s32[1024]{0:T(1024)} %param.11) | copy-start | bytes 12292
  101.3 7.9 %copy-start.12 = (bf16[1024,2048]{1,0:T(8,128)(2,1)S(1)}, bf16[1024,2048]{1,0:T(8,128)(2,1)}, u32[]{:S(2)}) copy-start(bf16[1024,2048]{1,0:T(8,128)(2,1)} %get-tuple-element.26) | copy-start | bytes 12582916
  116.5 312.2 %reduce-scatter.3.cloned.1.call-start = ((), (), s32[]{:S(2)}) async-start(), calls=%async_computation.3 | async-start | bytes 10485760 | tf_op jit(solution)/shard_map/reduce_scatter | solution.py:483
  182.9 247.1 %copy-start.6 = (f32[2048,256]{1,0:T(8,128)S(1)}, f32[2048,256]{1,0:T(8,128)}, u32[]{:S(2)}) copy-start(f32[2048,256]{1,0:T(8,128)} %get-tuple-element.29.tab_ref) | copy-start | bytes 6291460
  182.9 247.1 %copy-start.8 = (f32[128,128]{1,0:T(8,128)S(1)}, f32[128,128]{1,0:T(8,128)}, u32[]{:S(2)}) copy-start(f32[128,128]{1,0:T(8,128)} %constant.98.clone) | copy-start | bytes 196612
  325.2 223.2 %reduce-scatter.5.cloned.1.call-start = ((), (), s32[]{:S(2)}) async-start(), calls=%async_computation.4 | async-start | bytes 13107200 | tf_op jit(solution)/shard_map/reduce_scatter | solution.py:488
  455.0 93.5 %copy-start.10 = (bf16[2048]{0:T(1024)(128)(2,1)S(1)}, bf16[2048]{0:T(1024)(128)(2,1)}, u32[]{:S(2)}) copy-start(bf16[2048]{0:T(1024)(128)(2,1)} %param.12) | copy-start | bytes 12292
  455.1 201.0 %all-gather.3.cloned.1.call-start = ((), (), s32[]{:S(2)}) async-start(), calls=%async_computation.5 | async-start | bytes 23592960 | tf_op jit(solution)/shard_map/all_gather | solution.py:489
  548.4 37.7 %collective-permute-start.4 = (f32[1024,2048]{1,0:T(8,128)}, f32[1024,2048]{1,0:T(8,128)}, u32[]{:S(2)}, u32[]{:S(2)}) collective-permute-start(f32[1024,2048]{1,0:T(8,128)} %all-reduce.2.cloned.1.call-done), channel_id=1, source_target_pairs={{0,1},{1,0},{2,3},{3,2},{4,5},{5,4},{6,7},{7,6},{8,9},{9,8},{10,11... | collective-permute-start | bytes 25165832 | tf_op jit(solution)/shard_map/ppermute | solution.py:443
  550.3 23.7 %collective-permute-start.1 = (bf16[1024,1024]{1,0:T(8,128)(2,1)S(1)}, bf16[1024,1024]{1,0:T(8,128)(2,1)}, u32[]{:S(2)}, u32[]{:S(2)}) collective-permute-start(bf16[1024,1024]{1,0:T(8,128)(2,1)S(1)} %slice.104), channel_id=1, source_target_pairs={{0,1},{1,0},{2,3},{3,2},{4,5},{5,4},{6,7},{7,6},{8,9},{9,8},{10,11... | collective-permute-start | bytes 6291464 | tf_op jit(solution)/shard_map/ppermute | solution.py:443
  556.7 8.0 %copy-start.5 = (bf16[2048,1024]{1,0:T(8,128)(2,1)S(1)}, bf16[2048,1024]{1,0:T(8,128)(2,1)}, u32[]{:S(2)}) copy-start(bf16[2048,1024]{1,0:T(8,128)(2,1)} %get-tuple-element.24) | copy-start | bytes 12582916
  564.7 9.4 %copy-start = (bf16[1024,2048]{1,0:T(8,128)(2,1)S(1)}, bf16[1024,2048]{1,0:T(8,128)(2,1)}, u32[]{:S(2)}) copy-start(bf16[1024,2048]{1,0:T(8,128)(2,1)} %hid.1) | copy-start | bytes 12582916
  564.7 21.4 %slice-start.2 = ((s8[8388608]{0:T(1024)(128)(4,1)}), s8[4194304]{0:T(1024)(128)(4,1)S(1)}, s32[]{:S(2)}) async-start(s8[8388608]{0:T(1024)(128)(4,1)} %bitcast.69), calls=%async_computation.8 | async-start | bytes 8388608
  564.7 34.6 %slice-start = ((s8[5242880]{0:T(1024)(128)(4,1)}), s8[4194304]{0:T(1024)(128)(4,1)S(1)}, s32[]{:S(2)}) async-start(s8[5242880]{0:T(1024)(128)(4,1)} %bitcast.67), calls=%async_computation.6 | async-start | bytes 8388608
  574.0 12.1 %slice-start.3 = ((s8[8388608]{0:T(1024)(128)(4,1)}), s8[4194304]{0:T(1024)(128)(4,1)S(1)}, s32[]{:S(2)}) async-start(s8[8388608]{0:T(1024)(128)(4,1)} %bitcast.69), calls=%async_computation.9 | async-start | bytes 8388608
  574.0 25.3 %slice-start.1 = ((s8[5242880]{0:T(1024)(128)(4,1)}), s8[1048576]{0:T(1024)(128)(4,1)S(1)}, s32[]{:S(2)}) async-start(s8[5242880]{0:T(1024)(128)(4,1)} %bitcast.67), calls=%async_computation.7 | async-start | bytes 2097152
  608.6 11.5 %collective-permute-start.3 = (f32[1280]{0:T(1024)S(1)}, f32[1280]{0:T(1024)S(1)}, u32[]{:S(2)}, u32[]{:S(2)}) collective-permute-start(f32[1280]{0:T(1024)S(1)} %psum.23), channel_id=1, source_target_pairs={{0,1},{1,0},{2,3},{3,2},{4,5},{5,4},{6,7},{7,6},{8,9},{9,8},{10,11... | collective-permute-start | bytes 15368 | tf_op jit(solution)/shard_map/ppermute | solution.py:443
  608.7 11.7 %collective-permute-start.2 = (bf16[1024,1280]{1,0:T(8,128)(2,1)S(1)}, bf16[1024,1280]{1,0:T(8,128)(2,1)S(1)}, u32[]{:S(2)}, u32[]{:S(2)}) collective-permute-start(bf16[1024,1280]{1,0:T(8,128)(2,1)S(1)} %slice.132), channel_id=1, source_target_pairs={{0,1},{1,0},{2,3},{3,2},{4,5},{5,4},{6,7},{7,6},{8,9},{9,8},{10,11... | collective-permute-start | bytes 7864328 | tf_op jit(solution)/shard_map/ppermute | solution.py:443
  609.3 11.0 %copy-start.1 = (bf16[1024,2048]{1,0:T(8,128)(2,1)S(1)}, bf16[1024,2048]{1,0:T(8,128)(2,1)}, u32[]{:S(2)}) copy-start(bf16[1024,2048]{1,0:T(8,128)(2,1)} %hid.1) | copy-start | bytes 12582916
  609.3 11.0 %copy-start.3 = (bf16[2048,1024]{1,0:T(8,128)(2,1)S(1)}, bf16[2048,1024]{1,0:T(8,128)(2,1)}, u32[]{:S(2)}) copy-start(bf16[2048,1024]{1,0:T(8,128)(2,1)} %get-tuple-element.52) | copy-start | bytes 12582916
  609.3 11.0 %copy-start.7 = (bf16[2048,128]{1,0:T(8,128)(2,1)S(1)}, bf16[2048,128]{1,0:T(8,128)(2,1)}, u32[]{:S(2)}) copy-start(bf16[2048,128]{1,0:T(8,128)(2,1)} %get-tuple-element.57) | copy-start | bytes 1572868
  620.3 11.5 %copy-start.11 = (f32[2560]{0:T(1024)}, f32[2560]{0:T(1024)S(1)}, u32[]{:S(2)}) copy-start(f32[2560]{0:T(1024)S(1)} %slice_dynamic-update-slice_fusion.2) | copy-start | bytes 30724
  (2 other events, 10.2 us)
Sparse Core Ops, SparseCore 0:
  116.7 208.4 all-reduce.1
  328.1 100.6 reduce-scatter.2
  455.2 93.1 reduce-scatter.4
  549.8 99.2 all-gather.2

commit v2 on v1

--- a/solution.py
+++ b/solution.py
@@ -19,7 +19,7 @@
 SCALE = HD ** -0.5
 CL2 = math.log2(math.e) * SCALE
 f32, bf16 = jnp.float32, jnp.bfloat16
-BQ, BK, LOOK_F, LOOK_B = 256, 256, 7, 4
+BQ, BK, LOOK_F, LOOK_B = 256, 256, 3, 4
 VR = HD + 16
 RISE = 60.0
 
@@ -31,14 +31,20 @@
 
 
 def visit_blocks(lo, hi, flo, fhi, block):
-    @pl.loop(flo, fhi)
-    def _(kb):
-        block(kb, False)
+    pairs = (fhi - flo) // 2
+
+    @pl.loop(0, pairs)
+    def _(j):
+        block((flo + 2 * j, flo + 2 * j + 1), False)
+
+    @pl.when(flo + 2 * pairs < fhi)
+    def _():
+        block((fhi - 1,), False)
 
     @pl.loop(0, (hi - lo) - (fhi - flo))
     def _(j):
         kb = lo + j
-        block(jnp.where(kb < flo, kb, kb + (fhi - flo)), True)
+        block((jnp.where(kb < flo, kb, kb + (fhi - flo)),), True)
 
 
 def fwd_kernel(meta, q_ref, do_ref, kv_ref, qi_ref, ds_ref, ctx_ref, lse_ref, dd_ref, vt_ref, qt, m_s, mx, acc, vmax, *, nh, piece):
@@ -71,15 +77,16 @@
         kidx = kb * BK + lax.broadcasted_iota(jnp.int32, (BK, BQ), 0)
         return (kidx >= ds_ref[...]) & (kidx <= qi_ref[...])
 
-    def heads(score, soft, pv):
+    def units(n_units, score, soft, pv):
+        la = LOOK_F if n_units > nh else nh - 1
         sc, pb = {}, {}
-        for t in range(nh + LOOK_F + 1):
-            if t < nh:
+        for t in range(n_units + la + 1):
+            if t < n_units:
                 sc[t] = score(t)
-            if t >= LOOK_F + 1:
-                pv(t - LOOK_F - 1, pb.pop(t - LOOK_F - 1))
-            if LOOK_F <= t < nh + LOOK_F:
-                pb[t - LOOK_F] = soft(t - LOOK_F, sc.pop(t - LOOK_F))
+            if t >= la + 1:
+                pv(t - la - 1, pb.pop(t - la - 1))
+            if la <= t < n_units + la:
+                pb[t - la] = soft(t - la, sc.pop(t - la))
 
     def first(kb):
         kblk, vt = load(kb)
@@ -97,25 +104,26 @@
         def pv(h, p):
             acc[h] = jnp.dot(vt, p, preferred_element_type=f32)
 
-        heads(score, soft, pv)
-
-    def block(kb, masked):
-        kblk, vt = load(kb)
-        msk = visible(kb) if masked else None
-
-        def score(h):
-            return jnp.dot(kblk, qt[h], preferred_element_type=f32) * CL2
-
-        def soft(h, s):
+        units(nh, score, soft, pv)
+
+    def block(kbs, masked):
+        kv = [load(kb) for kb in kbs]
+        msk = visible(kbs[0]) if masked else None
+
+        def score(u):
+            return jnp.dot(kv[u // nh][0], qt[u % nh], preferred_element_type=f32) * CL2
+
+        def soft(u, s):
+            h = u % nh
             if masked:
                 s = jnp.where(msk, s, 2 * NEG)
             mx[h] = jnp.maximum(mx[h], jnp.max(s.reshape(BK // 8, 8, BQ), axis=0))
             return jnp.exp2(s - m_s[h:h + 1, :]).astype(bf16)
 
-        def pv(h, p):
-            acc[h] += jnp.dot(vt, p, preferred_element_type=f32)
-
-        heads(score, soft, pv)
+        def pv(u, p):
+            acc[u % nh] += jnp.dot(kv[u // nh][1], p, preferred_element_type=f32)
+
+        units(nh * len(kbs), score, soft, pv)
 
     first(hi - 1)
     visit_blocks(lo, hi - 1, jnp.minimum(flo, jnp.minimum(fhi, hi - 1)), jnp.minimum(fhi, hi - 1), block)
@@ -178,8 +186,11 @@
                    jax.ShapeDtypeStruct((nh, t), f32)])(meta, q, do, kv, qi, ds)
 
 
-def bwd_kernel(meta, q_ref, do_ref, kv_ref, qi_ref, ds_ref, lse_ref, dd_ref, tab_ref,
-               dq_ref, dkv_ref, kt_ref, qt, dot_, dqa, *, nh, piece):
+def bwd_kernel(meta, q_ref, do_ref, kv_ref, qi_ref, ds_ref, lse_ref, dd_ref, *rest, nh, piece, near):
+    if near:
+        tab_ref, dq_in, dq_ref, dkv_ref, kt_ref, qt, dot_, dqa = rest
+    else:
+        dqa, dkv_ref, kt_ref, qt, dot_ = rest
     i = pl.program_id(0)
     swap = meta[4, 0]
 
@@ -195,17 +206,15 @@
     for h in range(nh):
         qt[h] = q_ref[:, h * HD:(h + 1) * HD].T
         dot_[h] = do_ref[:, h * HD:(h + 1) * HD].T
-    dqa[...] = jnp.zeros_like(dqa)
-
-    def block(kb, masked):
-        off = pl.multiple_of(store_off(kb, BK, swap, piece), BK)
-        kblk = kv_ref[pl.ds(off, BK), :HD]
-        kt = kt_ref[:, pl.ds(off, BK)]
-        vblk = kv_ref[pl.ds(off, BK), HD:]
+    dqa[...] = dq_in[...] if near else jnp.zeros_like(dqa)
+
+    def block(kbs, masked):
+        base = meta[5, 0] * (2 * piece) if near else 0
+        at = [pl.ds(pl.multiple_of(store_off(kb, BK, swap, piece) - base, BK), BK) for kb in kbs]
         if masked:
-            kidx = kb * BK + lax.broadcasted_iota(jnp.int32, (BK, BQ), 0)
+            kidx = kbs[0] * BK + lax.broadcasted_iota(jnp.int32, (BK, BQ), 0)
             msk = (kidx >= ds_ref[...]) & (kidx <= qi_ref[...])
-        acc = [None, None]
+        acc = {}
 
         def mid(h, s, dp):
             p = jnp.exp2(s * CL2 - lse_ref[h:h + 1, :])
@@ -213,50 +222,63 @@
                 p = jnp.where(msk, p, 0.0)
             return p.astype(bf16), (p * (dp - dd_ref[h:h + 1, :])).astype(bf16)
 
+        def add(key, v):
+            acc[key] = v if key not in acc else acc[key] + v
+
         sc, pa = {}, {}
-        for t in range(nh + LOOK_B + 1):
-            if t < nh:
-                sc[t] = (jnp.dot(kblk, qt[t], preferred_element_type=f32),
-                         jnp.dot(vblk, dot_[t], preferred_element_type=f32))
+        n_units = nh * len(kbs)
+        for t in range(n_units + LOOK_B + 1):
+            if t < n_units:
+                b, h = divmod(t, nh)
+                sc[t] = (jnp.dot(kv_ref[at[b], :HD], qt[h], preferred_element_type=f32),
+                         jnp.dot(kv_ref[at[b], HD:], dot_[h], preferred_element_type=f32))
             u = t - LOOK_B - 1
             if u >= 0:
+                b, h = divmod(u, nh)
                 pb, dsb = pa.pop(u)
-                t1 = jnp.dot(pb, do_ref[:, u * HD:(u + 1) * HD], preferred_element_type=f32)
-                t2 = jnp.dot(dsb, q_ref[:, u * HD:(u + 1) * HD], preferred_element_type=f32)
-                acc[0] = t1 if acc[0] is None else acc[0] + t1
-                acc[1] = t2 if acc[1] is None else acc[1] + t2
-                dqa[u] += jnp.dot(kt, dsb, preferred_element_type=f32)
-            if LOOK_B <= t < nh + LOOK_B:
-                pa[t - LOOK_B] = mid(t - LOOK_B, *sc.pop(t - LOOK_B))
-        dkv_ref[pl.ds(off, BK), :HD] += acc[1]
-        dkv_ref[pl.ds(off, BK), HD:] += acc[0]
-
-    visit_blocks(meta[0, i], meta[1, i], meta[2, i], meta[3, i], block)
-    ct = tab_ref[:, :HD].T
-    even = lax.broadcasted_iota(jnp.int32, (HD, BQ), 0) % 2 == 0
-    st = jnp.where(even, tab_ref[:, HD:].T, -tab_ref[:, HD:].T)
-    for h in range(nh):
-        g = dqa[h] * SCALE
-        part = jnp.where(even, pltpu.roll(g, HD - 1, 0), pltpu.roll(g, 1, 0))
-        dq_ref[:, h * HD:(h + 1) * HD] = (g * ct + part * st).T.astype(bf16)
-
-
-def flash_bwd(meta, q, do, kv, qi, ds, lse, dd, tab, piece):
+                add((b, 1), jnp.dot(pb, do_ref[:, h * HD:(h + 1) * HD], preferred_element_type=f32))
+                add((b, 0), jnp.dot(dsb, q_ref[:, h * HD:(h + 1) * HD], preferred_element_type=f32))
+                dqa[h] += jnp.dot(kt_ref[:, at[b]], dsb, preferred_element_type=f32)
+            if LOOK_B <= t < n_units + LOOK_B:
+                pa[t - LOOK_B] = mid((t - LOOK_B) % nh, *sc.pop(t - LOOK_B))
+        for b in range(len(kbs)):
+            dkv_ref[at[b], :HD] += acc[b, 0]
+            dkv_ref[at[b], HD:] += acc[b, 1]
+
+    split = meta[5, 0] * (2 * piece // BK)
+    clip = (lambda v: jnp.maximum(v, split)) if near else (lambda v: jnp.minimum(v, split))
+    visit_blocks(*[clip(meta[r, i]) for r in range(4)], block)
+    if near:
+        ct = tab_ref[:, :HD].T
+        even = lax.broadcasted_iota(jnp.int32, (HD, BQ), 0) % 2 == 0
+        st = jnp.where(even, tab_ref[:, HD:].T, -tab_ref[:, HD:].T)
+        for h in range(nh):
+            g = dqa[h] * SCALE
+            part = jnp.where(even, pltpu.roll(g, HD - 1, 0), pltpu.roll(g, 1, 0))
+            dq_ref[:, h * HD:(h + 1) * HD] = (g * ct + part * st).T.astype(bf16)
+
+
+def flash_bwd(meta, q, do, kv, qi, ds, lse, dd, piece, tab=None, dq=None):
+    near = tab is not None
     t, w = q.shape
     nh = w // HD
-    nk = kv.shape[0]
+    nk = 2 * piece if near else kv.shape[0]
     tok = pl.BlockSpec((BQ, w), lambda i, m: (i, 0))
+    dqs = pl.BlockSpec((None, nh, HD, BQ), lambda i, m: (i, 0, 0, 0))
+    keys = pl.BlockSpec((nk, 2 * HD), lambda i, m: (m[5, 0] if near else 0, 0), pipeline_mode=pl.Buffered(1))
+    part = jax.ShapeDtypeStruct((t // BQ, nh, HD, BQ), f32)
     gs = pltpu.PrefetchScalarGridSpec(
         num_scalar_prefetch=1, grid=(t // BQ,),
-        in_specs=[tok, tok, resident((nk, 2 * HD)), rows_spec(1), rows_spec(1),
-                  rows_spec(nh), rows_spec(nh), pl.BlockSpec((BQ, 2 * HD), lambda i, m: (i, 0))],
-        out_specs=[tok, resident((nk, 2 * HD))],
-        scratch_shapes=[pltpu.VMEM((HD, nk), bf16), pltpu.VMEM((nh, HD, BQ), bf16), pltpu.VMEM((nh, HD, BQ), bf16), pltpu.VMEM((nh, HD, BQ), f32)])
+        in_specs=[tok, tok, keys, rows_spec(1), rows_spec(1), rows_spec(nh), rows_spec(nh)]
+        + ([pl.BlockSpec((BQ, 2 * HD), lambda i, m: (i, 0)), dqs] if near else []),
+        out_specs=[tok if near else dqs, resident((nk, 2 * HD))],
+        scratch_shapes=[pltpu.VMEM((HD, nk), bf16), pltpu.VMEM((nh, HD, BQ), bf16), pltpu.VMEM((nh, HD, BQ), bf16)]
+        + ([pltpu.VMEM((nh, HD, BQ), f32)] if near else []))
     return pl.pallas_call(
-        functools.partial(bwd_kernel, nh=nh, piece=piece), grid_spec=gs, name='flash_bwd',
-        cost_estimate=pl.CostEstimate(flops=10 * t * t * w, bytes_accessed=t * w * 8, transcendentals=0),
-        out_shape=[jax.ShapeDtypeStruct((t, w), bf16), jax.ShapeDtypeStruct((nk, 2 * HD), f32)],
-    )(meta, q, do, kv, qi, ds, lse, dd, tab)
+        functools.partial(bwd_kernel, nh=nh, piece=piece, near=near), grid_spec=gs, name='flash_bwd_' + ('near' if near else 'far'),
+        cost_estimate=pl.CostEstimate(flops=(4 if near else 7) * t * t * w, bytes_accessed=t * w * 8, transcendentals=0),
+        out_shape=[jax.ShapeDtypeStruct((t, w), bf16) if near else part, jax.ShapeDtypeStruct((nk, 2 * HD), f32)],
+    )(meta, q, do, kv, qi, ds, lse, dd, *((tab, dq) if near else ()))
 
 
 MESH = pl.DeviceIdType.MESH
@@ -411,13 +433,13 @@
     )(hidden, grad_out, tab, norm_gain, bias, rot, w_qkv, w_out)
 
 
-def block_table(qi, ds, swap):
+def block_table(qi, ds, swap, chip):
     q2, d2 = qi.reshape(-1, BQ), ds.reshape(-1, BQ)
     lo = d2[:, 0] // BK
     hi = q2[:, -1] // BK + 1
     flo = jnp.minimum((d2[:, -1] + BK - 1) // BK, hi)
     fhi = jnp.maximum((q2[:, 0] + 1) // BK, flo)
-    return jnp.stack([lo, hi, flo, fhi, jnp.full_like(lo, swap)]).astype(jnp.int32)
+    return jnp.stack([lo, hi, flo, fhi, jnp.full_like(lo, swap), jnp.full_like(lo, chip)]).astype(jnp.int32)
 
 
 def pair_swap():
@@ -442,16 +464,13 @@
         x, k = lax.axis_index('x'), lax.axis_index('k')
         other = lambda a: lax.ppermute(a, 'k', flip)
         both = lambda a: jnp.concatenate([a, other(a)], axis=0)
+        ordered = lambda a, b: jnp.where(k == 0, jnp.concatenate([a, b], axis=1), jnp.concatenate([b, a], axis=1))
 
         pos2 = both(doc_pos)
         base = x * (CORES * n)
         qi = jnp.concatenate([base + k * n + jnp.arange(n), base + (1 - k) * n + jnp.arange(n)]).astype(jnp.int32)
         ds = qi - pos2
-        meta = block_table(qi, ds, k)
-
-        def cols(w, c):
-            part = lambda a, b: lax.dynamic_slice_in_dim(w, a, b, axis=-1)
-            return jnp.concatenate([part(c * aw, aw), part(att + c * kw, kw), part(att + kvw + c * kw, kw)], axis=-1)
+        meta = block_table(qi, ds, k, x)
 
         inv_freq = ROPE_BASE ** (-jnp.arange(0, ROT_DIMS, 2).astype(f32) / ROT_DIMS)
         ang = inv_freq[:, None] * doc_pos.astype(f32)[None, :]
@@ -462,57 +481,59 @@
         gain = norm_gain.astype(f32)
         normed, go_o, q, gctx, kv_all, tab2 = front(hidden, grad_out, tab, norm_gain[None], bias,
                                                      jnp.asarray(pair_swap(), bf16), w_qkv, w_out, nx, kw)
-        w_me, w_ot = cols(w_qkv, k), cols(w_qkv, 1 - k)
-        wo_me = lax.dynamic_slice_in_dim(w_out, k * aw, aw, axis=0)
-        wo_ot = lax.dynamic_slice_in_dim(w_out, (1 - k) * aw, aw, axis=0)
         ctx, lse, dd = flash_fwd(meta, q, gctx, kv_all, qi[None], ds[None], n)
         over = (((0,), (0,)), ((), ()))
         g_wout = (lax.dot_general(ctx[:n], grad_out, over, preferred_element_type=f32)
                   + lax.dot_general(ctx[n:], go_o, over, preferred_element_type=f32))
         lse, g_wout = lax.optimization_barrier((lse, g_wout))
         g_wout = lax.psum(g_wout, 'x')
-        ctx_o = other(ctx[n:])
-        y_out = (hidden.astype(f32) + jnp.dot(ctx[:n], wo_me, preferred_element_type=f32)
-                 + jnp.dot(ctx_o, wo_ot, preferred_element_type=f32)).astype(bf16)
-
-        dq, dkv = flash_bwd(meta, q, gctx, kv_all, qi[None], ds[None], lse, dd, tab2, n)
+        back = functools.partial(flash_bwd, meta, q, gctx, kv_all, qi[None], ds[None], lse, dd, n)
+        dq_far, dkv = back()
         c_tok, s_tok = tab2[:, :HD], tab2[:, HD:]
-        dkv, g_wout = lax.optimization_barrier((dkv, g_wout))
+        dkv, g_wout, dq_far = lax.optimization_barrier((dkv, g_wout, dq_far))
+        dkv = lax.psum_scatter(dkv, 'x', scatter_dimension=0, tiled=True)
+        dq, dkv_near = back(tab2, dq_far)
+        dq, ctx = lax.optimization_barrier((dq, ctx))
+        g_wq = lax.dot_general(normed, dq, over, preferred_element_type=f32)
         wout_o = other(g_wout)
+        dq_all = ordered(dq[:n], other(dq[n:]))
+        rows = (((1,), (1,)), ((), ()))
+        gnorm = lax.dot_general(dq_all, w_qkv[:, :att], rows, preferred_element_type=f32)
         o_wout = jnp.where(k == 0, jnp.concatenate([g_wout, wout_o]), jnp.concatenate([wout_o, g_wout]))
-        dkv = lax.psum_scatter(dkv, 'x', scatter_dimension=0, tiled=True)
+        ctx_all = ordered(ctx[:n], other(ctx[n:]))
+        y_out = (hidden.astype(f32) + jnp.dot(ctx_all, w_out, preferred_element_type=f32)).astype(bf16)
+        g_wq, dkv = lax.optimization_barrier((g_wq, dkv))
+        g_wq = lax.psum_scatter(g_wq, 'x', scatter_dimension=0, tiled=True)
+        dkv = dkv + dkv_near
         dk = dkv[:, :kw] * SCALE
         dkt = jnp.dot(dk, jnp.asarray(pair_swap().T), precision=lax.Precision.HIGHEST, preferred_element_type=f32)
-        gqkv = jnp.concatenate([dq, (dk * c_tok + dkt * s_tok).astype(bf16), dkv[:, kw:].astype(bf16)], axis=1)
-        g_wqkv = lax.dot_general(normed, gqkv, (((0,), (0,)), ((), ())), preferred_element_type=f32)
-        g_wqkv = lax.psum_scatter(g_wqkv, 'x', scatter_dimension=0, tiled=True)
-        g_wqkv = lax.all_gather(g_wqkv, ('x', 'k'), axis=0)
-        g_wqkv = g_wqkv.reshape(-1, CORES, *g_wqkv.shape[1:])
-        two = lambda a, b: [g_wqkv[:, c, :, a:b] for c in range(CORES)]
-        o_wqkv = jnp.concatenate(two(0, aw) + two(aw, aw + kw) + two(aw + kw, aw + 2 * kw), axis=-1).reshape(w_qkv.shape)
-        gq_o = other(gqkv[n:])
-        dims = (((1,), (1,)), ((), ()))
-        gnorm = (lax.dot_general(gqkv[:n], w_me, dims, preferred_element_type=f32)
-                 + lax.dot_general(gq_o, w_ot, dims, preferred_element_type=f32))
+        gkv = jnp.concatenate([(dk * c_tok + dkt * s_tok).astype(bf16), dkv[:, kw:].astype(bf16)], axis=1)
+        g_wkv = lax.dot_general(normed, gkv, over, preferred_element_type=f32)
+        gkv_o = other(gkv[n:])
+        gkv_all = jnp.concatenate([ordered(gkv[:n, :kw], gkv_o[:, :kw]), ordered(gkv[:n, kw:], gkv_o[:, kw:])], axis=1)
+        gnorm = gnorm + lax.dot_general(gkv_all, w_qkv[:, att:], rows, preferred_element_type=f32)
         h32 = hidden.astype(f32)
         inv_rms = lax.rsqrt(jnp.mean(h32 * h32, axis=-1, keepdims=True) + EPS_NORM)
         x_hat = h32 * inv_rms
-        g_gain = jnp.sum(gnorm * x_hat, axis=0)
         scaled = gnorm * gain
         g_hidden = (grad_out.astype(f32) + inv_rms * (scaled - x_hat * jnp.mean(scaled * x_hat, axis=-1, keepdims=True))).astype(bf16)
-        g_b = jnp.sum(gqkv.astype(f32), axis=0)
-        g_gain = lax.psum(g_gain, ('x', 'k'))
-        g_b = lax.psum(g_b, 'x')
-
-        def join(out, mine, c):
-            put = lambda o, v, at: lax.dynamic_update_slice_in_dim(o, v, at, axis=-1)
-            out = put(out, mine[..., :aw], c * aw)
-            out = put(out, mine[..., aw:aw + kw], att + c * kw)
-            return put(out, mine[..., aw + kw:], att + kvw + c * kw)
-
-        full = lambda shape: jnp.zeros(shape, f32)
-        o_b = join(join(full(b_qkv.shape), g_b, k), other(g_b), 1 - k)
-        return y_out, g_hidden, g_gain, o_wqkv, o_b, o_wout
+        total = lambda a: jnp.sum(a.astype(f32), axis=0)
+        sums = jnp.concatenate([total(gnorm * x_hat), total(dq_all), total(gkv_all)])
+        srows = -(-sums.size // (2 * kw))
+        sums = jnp.pad(sums, (0, srows * 2 * kw - sums.size)).reshape(srows, 2 * kw)
+        g_wkv, g_wq, sums, g_hidden = lax.optimization_barrier((g_wkv, g_wq, sums, g_hidden))
+        g_wkv = lax.psum_scatter(g_wkv, 'x', scatter_dimension=0, tiled=True)
+        g_wq, g_wkv = lax.optimization_barrier((g_wq, g_wkv))
+        by_chip = lambda g: lax.all_gather(g, ('x', 'k'), axis=0).reshape(nx, CORES, *g.shape)
+        g_wq = by_chip(g_wq)
+        g_wkv, g_wq, y_out, o_wout = lax.optimization_barrier((g_wkv, g_wq, y_out, o_wout))
+        o_q = jnp.concatenate([g_wq[:, c] for c in range(CORES)], axis=-1).reshape(d, att)
+        last = by_chip(jnp.concatenate([g_wkv, sums]))
+        g_wkv = last[:, :, :d // nx]
+        sums = jnp.sum(last[:, :, d // nx:], axis=(0, 1)).reshape(-1)
+        o_kv = jnp.concatenate([g_wkv[:, c, :, p * kw:(p + 1) * kw] for p in range(2) for c in range(CORES)], axis=-1)
+        o_wqkv = lax.dynamic_update_slice(jnp.pad(o_q, ((0, 0), (0, 2 * kvw))), o_kv.reshape(d, 2 * kvw), (0, att))
+        return y_out, g_hidden, sums[:d], o_wqkv, sums[d:d + b_qkv.size], o_wout
 
     act = P(('dp', 'x', 'k'), None)
     row = P(('dp', 'x', 'k'))

time: 680 us -> 651 us (0.957)
  waiting for transfers between devices: 339 us -> 364 us
  blocking collectives: 24.6 us -> 0 us
  Pallas kernels: 151 us -> 135 us
    reduce_scatter x1, waiting for transfers between devices: 103 us -> 33.8 us  [per_device(): dkv = lax.psum_scatter(dkv, 'x', scatter_dimension=0, tiled=True)]
    psum x1, waiting for transfers between devices: 142 us -> 210 us  [per_device(): g_wout = lax.psum(g_wout, 'x')]
    all_gather x1 -> x2, waiting for transfers between devices: 0.01 us -> 50.9 us  [per_device(): lax.all_gather(g, ('x', 'k'), axis=0).reshape(nx, CORES, *g.shape)]
    reduce_scatter x1 -> x2, waiting for transfers between devices: 93.2 us -> 52.4 us  [the longest x1 27.9 us: per_device(): g_wkv = lax.psum_scatter(g_wkv, 'x', scatter_dimension=0, tiled=True)]
    psum x2 -> x0, blocking collectives: 24.6 us -> none  [the longest x1 15.6 us: per_device(): g_gain = lax.psum(g_gain, ('x', 'k'))]
    ppermute x5, waiting for transfers between devices: 0.01 us -> 16.9 us  [per_device(): other = lambda a: lax.ppermute(a, 'k', flip)]
    dynamic_slice x2 -> x0, local copies, waits for them, and re-layouts: 10.7 us -> none  [cols(): part = lambda a, b: lax.dynamic_slice_in_dim(w, a, b, axis=-1)]
    pallas_call x1, Pallas kernels: 37.5 us -> 28.7 us  [flash_fwd(): pl.pallas_call(functools.partial(fwd_kernel, nh=nh, piece=piece), grid_sp...]
  transfers between devices with their start and end apart: 9 -> 11, of which waited for: 3 -> 8; matrix products, arithmetic and copies ran while one was open for 13% -> 18% of each run, Pallas kernels for 17% -> 16%
where the time goes in v2:
time: 651 us; the launch traced here: 663 us
  waiting for transfers between devices  364 us (56%)
  Pallas kernels  135 us (21%)
  matrix products  72.9 us (11%)
  local copies, waits for them, and re-layouts  38.3 us (6%)
  other arithmetic  36.2 us (6%)
  between operations  15 us (2%)
    psum x1, waiting for transfers between devices, per_device(): g_wout = lax.psum(g_wout, 'x')  210 us
    pallas_call x2, Pallas kernels, flash_bwd(): pl.pallas_call(functools.partial(bwd_kernel, nh=nh, piece=piece, near=nea...  58.8 us
    all_gather x2, waiting for transfers between devices, per_device(): lax.all_gather(g, ('x', 'k'), axis=0).reshape(nx, CORES, *g.shape)  50.9 us
    pallas_call x1, Pallas kernels, front(): pl.pallas_call(functools.partial(front_kernel, n=n, nx=nx, aw=aw, kw=kw,...  47.2 us
    reduce_scatter x1, waiting for transfers between devices, per_device(): dkv = lax.psum_scatter(dkv, 'x', scatter_dimension=0, tiled=True)  33.8 us
    pallas_call x1, Pallas kernels, flash_fwd(): pl.pallas_call(functools.partial(fwd_kernel, nh=nh, piece=piece), grid_sp...  28.7 us
    reduce_scatter x1, waiting for transfers between devices, per_device(): g_wkv = lax.psum_scatter(g_wkv, 'x', scatter_dimension=0, tiled=True)  27.9 us
    reduce_scatter x1, waiting for transfers between devices, per_device(): g_wq = lax.psum_scatter(g_wq, 'x', scatter_dimension=0, tiled=True)  24.4 us
  transfers between devices with their start and end apart: 11, of which 8 were waited for; matrix products, arithmetic and copies ran while one was open for 18% of the time, Pallas kernels for 16%

profile of v2, /device:TPU:112, one launch (start us, length us, event | category | flops | bytes accessed | tf_op | source)
XLA Modules:
  0.0 662.6 jit_solution(3999827718269231876)
XLA Ops:
  14.3 47.2 %front.1 = (bf16[2048,2048]{1,0:T(8,128)(2,1)}, bf16[1024,2048]{1,0:T(8,128)(2,1)}, bf16[2048,1024]{1,0:T(8,128)(2,1)}, bf16[2048,1024]{1,0:T(8,128)(2,1)}, bf16...) custom-call(bf16[1024,2048]{1,0:T(8,128)(2,1)} %hid.1, bf16[1024,2048]{1,0:T(8,128)(2,1)} %go.1, ...), custom_call_target="tpu_custom_call" | custom-call | flops 60000002048 | bytes 50000000 | tf_op jit(solution)/shard_map/front/pallas_call | solution.py:422
  63.8 28.7 %flash_fwd.1 = (bf16[2048,1024]{1,0:T(8,128)(2,1)}, f32[8,2048]{1,0:T(8,128)}, f32[8,2048]{1,0:T(8,128)}) custom-call(s32[6,8]{1,0:T(8,128)} %stack.19.meta, bf16[2048,1024]{1,0:T(8,128)(2,1)} %get-tuple-element.39.q_ref, bf16[2048,1024]{1,0:T(8,128)(2,1)} %get-tuple-element.40.do_ref, bf16[8192,256]{1,0:T(8,128)(2,1)} %get-tuple-element.41.kv_ref, ...), custom_call_target="tpu_custom_call" | custom-call | flops 17179869184 | bytes 12582912 | tf_op jit(solution)/shard_map/flash_fwd/pallas_call | solution.py:182
  92.5 7.9 %fusion.28 = f32[1024,2048]{1,0:T(8,128)S(1)} fusion(bf16[1024,2048]{1,0:T(8,128)(2,1)} %go.1, bf16[2048,1024]{1,0:T(8,128)(2,1)} %get-tuple-element.62), kind=kOutput, calls=%fused_computation.36 | convolution fusion | flops 4294967296 | bytes 14680064 | tf_op jit(solution)/shard_map/dot_general | solution.py:486
  100.4 7.3 %convolution_add_fusion = f32[1024,2048]{1,0:T(8,128)} fusion(f32[1024,2048]{1,0:T(8,128)S(1)} %fusion.28, bf16[1024,2048]{1,0:T(8,128)(2,1)S(1)} %copy-done.9, bf16[2048,1024]{1,0:T(8,128)(2,1)S(1)} %copy-done.1), kind=kOutput, calls=%fused_computation.28 | convolution fusion | flops 4297064448 | bytes 23068672 | tf_op jit(solution)/shard_map/dot_general | solution.py:487
  107.9 16.7 %flash_bwd_far.1 = (f32[8,8,128,256]{3,2,1,0:T(8,128)}, f32[8192,256]{1,0:T(8,128)}) custom-call(s32[6,8]{1,0:T(8,128)} %stack.19.meta, bf16[2048,1024]{1,0:T(8,128)(2,1)} %get-tuple-element.39.q_ref, bf16[2048,1024]{1,0:T(8,128)(2,1)} %get-tuple-element.40.do_ref, bf16[8192,256]{1,0:T(8,128)(2,1)} %get-tuple-element.41.kv_ref, s32[1,2048]{1,0:T(1,128)} %bitcast.85, ...), custom_call_target="tpu_custom_call" | custom-call | flops 30064771072 | bytes 16777216 | tf_op jit(solution)/shard_map/flash_bwd_far/pallas_call | solution.py:277
  124.6 209.6 %all-reduce.2.cloned.1.call-done = f32[1024,2048]{1,0:T(8,128)} async-done(((f32[1024,2048]{1,0:T(8,128)}), f32[1024,2048]{1,0:T(8,128)}) %all-reduce.2.cloned.1.call-update) | async-done | bytes 8388624 | tf_op jit(solution)/shard_map/psum | solution.py:489
  334.4 42.1 %flash_bwd_near.1 = (bf16[2048,1024]{1,0:T(8,128)(2,1)}, f32[2048,256]{1,0:T(8,128)}) custom-call(s32[6,8]{1,0:T(8,128)} %stack.19.meta, bf16[2048,1024]{1,0:T(8,128)(2,1)} %get-tuple-element.39.q_ref, bf16[2048,1024]{1,0:T(8,128)(2,1)} %get-tuple-element.40.do_ref, bf16[8192,256]{1,0:T(8,128)(2,1)} %get-tuple-element.41.kv_ref, s32[1,2048]{1,0:T(1,128)} %bitcast.86, ...), custom_call_target="tpu_custom_call" | custom-call | flops 17179869184 | bytes 16777216 | tf_op jit(solution)/shard_map/flash_bwd_near/pallas_call | solution.py:277
  376.4 14.6 %fusion.61 = f32[2048,1024]{1,0:T(8,128)} fusion(bf16[2048,2048]{1,0:T(8,128)(2,1)} %get-tuple-element.38, bf16[2048,1024]{1,0:T(8,128)(2,1)} %get-tuple-element.53), kind=kOutput, calls=%fused_computation.124 | convolution fusion | flops 8589934592 | bytes 20971520 | tf_op jit(solution)/shard_map/dot_general | solution.py:497
  391.0 33.8 %reduce-scatter.4.cloned.1.call-done = f32[2048,256]{1,0:T(8,128)} async-done(((f32[8192,256]{1,0:T(8,128)}), f32[2048,256]{1,0:T(8,128)}) %reduce-scatter.4.cloned.1.call-update) | async-done | bytes 2097168 | tf_op jit(solution)/shard_map/reduce_scatter | solution.py:494
  425.0 4.0 fusion.57
  439.1 4.0 fusion.30
  444.7 7.4 %fusion.25 = f32[1024,2048]{1,0:T(8,128)} fusion(bf16[2048,2560]{1,0:T(8,128)(2,1)} %w_qkv.1, bf16[1024,256]{1,0:T(8,128)(2,1)S(1)} %maximum_select_fusion.8, bf16[1024,256]{1,0:T(8,128)(2,1)S(1)} %maximum_select_fusion.7), kind=kOutput, calls=%fused_computation.33 | convolution fusion | flops 2149580800 | bytes 11534336 | tf_op jit(solution)/shard_map/dot_general | solution.py:514
  452.1 17.9 %fusion.4 = (f32[1024]{0:T(1024)S(1)}, f32[2048]{0:T(1024)S(1)}, f32[1024,2048]{1,0:T(8,128)}) fusion(bf16[1024,2048]{1,0:T(8,128)(2,1)} %hid.1, f32[2048]{0:T(1024)S(1)} %convert_element_type.49, f32[1024]{0:T(1024)S(1)} %add_rsqrt_fusion, f32[1024,2048]{1,0:T(8,128)} %fusion.25, bf16[2048,2560]{1,0:T(8,128)(2,1)} %w_qkv.1, ...), kind=kOutput, calls=%fused_computation.8 | convolution fusion | flops 8625583104 | bytes 33579008 | tf_op jit(solution)/shard_map/dot_general | solution.py:501
  470.0 8.9 %fusion.8 = bf16[1024,2048]{1,0:T(8,128)(2,1)} fusion(bf16[1024,2048]{1,0:T(8,128)(2,1)} %hid.1, bf16[1024,2048]{1,0:T(8,128)(2,1)} %go.1, f32[1024,2048]{1,0:T(8,128)} %get-tuple-element.101, f32[1024]{0:T(1024)S(1)} %broadcast_multiply_fusion, f32[2048]{0:T(1024)S(1)} %convert_element_type.49, f32[1024]{0:T(1024)S(1)} %add_rsqrt_fusion), kind=kLoop, calls=%fused_computation.12 | loop fusion | flops 18874368 | bytes 20987904 | tf_op jit(solution)/shard_map/convert_element_type | solution.py:519
  479.0 24.4 %reduce-scatter.6.cloned.1.call-done = f32[512,1024]{1,0:T(8,128)} async-done(((f32[2048,1024]{1,0:T(8,128)}), f32[512,1024]{1,0:T(8,128)}) %reduce-scatter.6.cloned.1.call-update) | async-done | bytes 2097168 | tf_op jit(solution)/shard_map/reduce_scatter | solution.py:506
  503.5 27.9 %reduce-scatter.8.cloned.1.call-done = f32[512,256]{1,0:T(8,128)} async-done(((f32[2048,256]{1,0:T(8,128)}), f32[512,256]{1,0:T(8,128)}) %reduce-scatter.8.cloned.1.call-update) | async-done | bytes 524304 | tf_op jit(solution)/shard_map/reduce_scatter | solution.py:525
  535.2 16.1 %collective-permute-done.3 = bf16[1024,1024]{1,0:T(8,128)(2,1)S(1)} collective-permute-done((bf16[1024,1024]{1,0:T(8,128)(2,1)S(1)}, bf16[1024,1024]{1,0:T(8,128)(2,1)S(1)}, u32[]{:S(2)}, u32[]{:S(2)}) %collective-permute-start.3) | collective-permute-done | bytes 2097184 | tf_op jit(solution)/shard_map/ppermute | solution.py:465
  551.3 12.8 %fusion.10 = bf16[1024,2048]{1,0:T(8,128)(2,1)} fusion(bf16[1024,2048]{1,0:T(8,128)(2,1)S(1)} %copy-done, bf16[2048,2048]{1,0:T(8,128)(2,1)} %w_out.1, bf16[1024,1024]{1,0:T(8,128)(2,1)S(1)} %collective-permute-done.3, bf16[1024,1024]{1,0:T(8,128)(2,1)S(1)} %get-tuple-element.86, pred[]{:T(512)S(6)} %eq.2), kind=kOutput, calls=%fused_computation.14 | convolution fusion | flops 8615100416 | bytes 20971520 | tf_op jit(solution)/shard_map/dot_general | solution.py:504
  564.2 12.9 %maximum_select_fusion = f32[2048,2048]{1,0:T(8,128)} fusion(f32[1024,2048]{1,0:T(8,128)} %collective-permute-done.4, f32[1024,2048]{1,0:T(8,128)S(1)} %bitcast.73, pred[]{:T(512)S(6)} %eq.2), kind=kLoop, calls=%fused_computation | loop fusion | flops 12582912 | bytes 33554432 | tf_op jit(solution)/shard_map/jit(_where)/select_n | solution.py:502
  577.1 36.6 %all-gather.6.cloned.1.call-done = f32[4096,1024]{1,0:T(8,128)} async-done(((f32[512,1024]{1,0:T(8,128)}), f32[4096,1024]{1,0:T(8,128)}) %all-gather.6.cloned.1.call-update) | async-done | bytes 16777232 | tf_op jit(solution)/shard_map/all_gather | solution.py:527
  614.6 6.7 %fusion.54 = (f32[4,1,512,1024]{3,2,1,0:T(8,128)S(1)}, f32[4,1,512,1024]{3,2,1,0:T(8,128)S(1)}) fusion(f32[4,2,512,1024]{3,2,1,0:T(8,128)} %bitcast.71), kind=kLoop, calls=%fused_computation.117 | loop fusion | bytes 33554432 | tf_op jit(solution)/shard_map/slice | solution.py:530
  621.4 4.2 constant_dynamic-update-slice_fusion.5
  625.6 4.2 constant_dynamic-update-slice_fusion.4
  629.9 14.3 %all-gather.8.cloned.1.call-done = f32[8,530,256]{2,1,0:T(8,128)} async-done(((f32[1,530,256]{2,1,0:T(8,128)}), f32[8,530,256]{2,1,0:T(8,128)}) %all-gather.8.cloned.1.call-update) | async-done | bytes 4341776 | tf_op jit(solution)/shard_map/all_gather | solution.py:527
  (115 shorter events, 37.1 us)
Async XLA Ops:
  7.2 327.0 %all-reduce.2.cloned.1.call-start = ((), (), s32[]{:S(2)}) async-start(), calls=%async_computation.3 | async-start | bytes 16777216 | tf_op jit(solution)/shard_map/psum | solution.py:489
  7.2 55.0 %collective-permute-start = (s32[1024]{0:T(1024)}, s32[1024]{0:T(1024)S(1)}, u32[]{:S(2)}, u32[]{:S(2)}) collective-permute-start(s32[1024]{0:T(1024)} %param.11), channel_id=1, source_target_pairs={{0,1},{1,0},{2,3},{3,2},{4,5},{5,4},{6,7},{7,6},{8,9},{9,8},{10,11... | collective-permute-start | bytes 12296 | tf_op jit(solution)/shard_map/ppermute | solution.py:465
  14.3 47.8 %copy-start.7 = (s32[1024]{0:T(1024)S(1)}, s32[1024]{0:T(1024)}, u32[]{:S(2)}) copy-start(s32[1024]{0:T(1024)} %param.11) | copy-start | bytes 12292
  92.5 7.9 %copy-start.1 = (bf16[2048,1024]{1,0:T(8,128)(2,1)S(1)}, bf16[2048,1024]{1,0:T(8,128)(2,1)}, u32[]{:S(2)}) copy-start(bf16[2048,1024]{1,0:T(8,128)(2,1)} %get-tuple-element.62) | copy-start | bytes 12582916
  92.5 7.9 %copy-start.9 = (bf16[1024,2048]{1,0:T(8,128)(2,1)S(1)}, bf16[1024,2048]{1,0:T(8,128)(2,1)}, u32[]{:S(2)}) copy-start(bf16[1024,2048]{1,0:T(8,128)(2,1)} %get-tuple-element.44) | copy-start | bytes 12582916
  107.8 317.1 %reduce-scatter.4.cloned.1.call-start = ((), (), s32[]{:S(2)}) async-start(), calls=%async_computation.4 | async-start | bytes 10485760 | tf_op jit(solution)/shard_map/reduce_scatter | solution.py:494
  334.3 169.1 %reduce-scatter.6.cloned.1.call-start = ((), (), s32[]{:S(2)}) async-start(), calls=%async_computation.5 | async-start | bytes 10485760 | tf_op jit(solution)/shard_map/reduce_scatter | solution.py:506
  391.0 37.9 %copy-start.8 = (bf16[2048]{0:T(1024)(128)(2,1)S(1)}, bf16[2048]{0:T(1024)(128)(2,1)}, u32[]{:S(2)}) copy-start(bf16[2048]{0:T(1024)(128)(2,1)} %param.12) | copy-start | bytes 12292
  424.9 106.6 %reduce-scatter.8.cloned.1.call-start = ((), (), s32[]{:S(2)}) async-start(), calls=%async_computation.6 | async-start | bytes 2621440 | tf_op jit(solution)/shard_map/reduce_scatter | solution.py:525
  429.0 4.1 collective-permute-start.1
  429.0 7.9 %copy-start.2 = (f32[2048,256]{1,0:T(8,128)S(1)}, f32[2048,256]{1,0:T(8,128)}, u32[]{:S(2)}) copy-start(f32[2048,256]{1,0:T(8,128)} %reduce-scatter.4.cloned.1.call-done) | copy-start | bytes 6291460
  429.0 7.9 %copy-start.3 = (f32[2048,256]{1,0:T(8,128)S(1)}, f32[2048,256]{1,0:T(8,128)}, u32[]{:S(2)}) copy-start(f32[2048,256]{1,0:T(8,128)} %get-tuple-element.56) | copy-start | bytes 6291460
  429.0 8.3 %copy-start.5 = (f32[2048,256]{1,0:T(8,128)S(1)}, f32[2048,256]{1,0:T(8,128)}, u32[]{:S(2)}) copy-start(f32[2048,256]{1,0:T(8,128)} %get-tuple-element.47.rest_0_) | copy-start | bytes 6291460
  429.0 8.3 %copy-start.6 = (f32[128,128]{1,0:T(8,128)S(1)}, f32[128,128]{1,0:T(8,128)}, u32[]{:S(2)}) copy-start(f32[128,128]{1,0:T(8,128)} %constant.85.clone) | copy-start | bytes 196612
  433.1 5.7 slice-start.2
  438.5 4.6 collective-permute-start.2
  503.5 110.3 %all-gather.6.cloned.1.call-start = ((), (), s32[]{:S(2)}) async-start(), calls=%async_computation.7 | async-start | bytes 18874368 | tf_op jit(solution)/shard_map/all_gather | solution.py:527
  531.5 112.6 %all-gather.8.cloned.1.call-start = ((), (), s32[]{:S(2)}) async-start(), calls=%async_computation.8 | async-start | bytes 4939776 | tf_op jit(solution)/shard_map/all_gather | solution.py:527
  531.6 19.7 %copy-start = (bf16[1024,2048]{1,0:T(8,128)(2,1)S(1)}, bf16[1024,2048]{1,0:T(8,128)(2,1)}, u32[]{:S(2)}) copy-start(bf16[1024,2048]{1,0:T(8,128)(2,1)} %hid.1) | copy-start | bytes 12582916
  531.6 32.5 %collective-permute-start.4 = (f32[1024,2048]{1,0:T(8,128)}, f32[1024,2048]{1,0:T(8,128)}, u32[]{:S(2)}, u32[]{:S(2)}) collective-permute-start(f32[1024,2048]{1,0:T(8,128)} %all-reduce.2.cloned.1.call-done), channel_id=1, source_target_pairs={{0,1},{1,0},{2,3},{3,2},{4,5},{5,4},{6,7},{7,6},{8,9},{9,8},{10,11... | collective-permute-start | bytes 25165832 | tf_op jit(solution)/shard_map/ppermute | solution.py:465
  531.7 32.4 %slice-start = ((s8[8388608]{0:T(1024)(128)(4,1)}), s8[4194304]{0:T(1024)(128)(4,1)S(1)}, s32[]{:S(2)}) async-start(s8[8388608]{0:T(1024)(128)(4,1)} %bitcast.72), calls=%async_computation.9 | async-start | bytes 8388608
  534.6 16.7 %collective-permute-start.3 = (bf16[1024,1024]{1,0:T(8,128)(2,1)S(1)}, bf16[1024,1024]{1,0:T(8,128)(2,1)S(1)}, u32[]{:S(2)}, u32[]{:S(2)}) collective-permute-start(bf16[1024,1024]{1,0:T(8,128)(2,1)S(1)} %get-tuple-element.87), channel_id=1, source_target_pairs={{0,1},{1,0},{2,3},{3,2},{4,5},{5,4},{6,7},{7,6},{8,9},{9,8},{10,11... | collective-permute-start | bytes 6291464 | tf_op jit(solution)/shard_map/ppermute | solution.py:465
  551.3 12.8 %slice-start.1 = ((s8[8388608]{0:T(1024)(128)(4,1)}), s8[4194304]{0:T(1024)(128)(4,1)S(1)}, s32[]{:S(2)}) async-start(s8[8388608]{0:T(1024)(128)(4,1)} %bitcast.72), calls=%async_computation.10 | async-start | bytes 8388608
  564.1 49.6 %copy-start.4 = (f32[512,256]{1,0:T(8,128)S(1)}, f32[512,256]{1,0:T(8,128)}, u32[]{:S(2)}) copy-start(f32[512,256]{1,0:T(8,128)} %reduce-scatter.8.cloned.1.call-done) | copy-start | bytes 1572868
  (1 other events, 2.2 us)
Sparse Core Ops, SparseCore 0:
  107.9 226.2 all-reduce.1
  337.1 87.6 reduce-scatter.3
  427.2 76.1 reduce-scatter.5
  506.1 25.3 reduce-scatter.7
  532.9 80.7 all-gather.5
  615.1 28.9 all-gather.7
